TPU v7x, 32 devices: a whole 2x2x4 slice. The times are simulated.
32 devices in a mesh: row: 8 (over z, y), col: 4 (over x, core).
Axes of the slice: x: 2, y: 2, z: 4, core: 2. Of those that a mesh axis runs over, the one named last changes fastest.
Arguments:
- load_currents: float32 [32, 1024, 512], P(None, 'row', 'col'), may hold values from -36 to 36
- labels: int32 [1024, 512], P('row', 'col'), may hold values from 0 to 255, as said below
- bump_height: float32 [1024, 512], P('row', 'col'), may hold values from 0.5 to 2
- horizontal_class: int32 [1024, 512], P('row', 'col'), may hold values from 0 to 7
- vertical_class: int32 [1024, 512], P('row', 'col'), may hold values from 0 to 7
- pad_class: int32 [1024, 512], P('row', 'col'), may hold values from 0 to 7
- edge_table: float32 [8], replicated, may hold values from 0.5 to 4
- pad_table: float32 [8], replicated, may hold values from 0.02 to 0.5
Outputs:
- solution: float32 [32, 1024, 512], P(None, 'row', 'col')
- residual: float32 [32, 1024, 512], P(None, 'row', 'col')
Inputs may be any that keep to these rules, and one draw needn't show every extreme that they name: `labels`: every number from 0 to 255 is the label of some nodes; the label of node (i, j) is 16 * floor(16 * i2 / 1024) + floor(16 * j2 / 512) for some node (i2, j2) of the grid with |i2 - i| <= 16 and |j2 - j| <= 8.
All inputs are finite; a program needn't handle non-finite values.
Results may differ from a plain program's by a relative error of at most 0.0003.
Values sent between devices are 32-bit elements; how exact they have to be, the bound alone decides.
A program may use at most 128 MiB of HBM per device.

v0:
```python
import functools

import jax
import jax.numpy as jnp
from jax import lax
from jax.experimental import pallas as pl
from jax.experimental.pallas import tpu as pltpu
from jax.sharding import PartitionSpec as P

REG = 16
F32 = jnp.float32
precise = lax.Precision.HIGHEST
VM = pl.BlockSpec(memory_space=pltpu.VMEM)
PARAMS = pltpu.CompilerParams(vmem_limit_bytes=56 * 1024 * 1024)


def shape(*dims):
    return jax.ShapeDtypeStruct(dims, F32)


def sweep(size, out_ref):
    segment = 2 * REG
    for start in range(0, size, segment):
        reach = min(size, start + segment + 2 * REG)
        width = size
        lanes = lax.broadcasted_iota(jnp.int32, (reach, width), 1)
        rows = lax.broadcasted_iota(jnp.int32, (reach, 1), 0)
        row_lanes = lax.broadcasted_iota(jnp.int32, (1, width), 1)

        def step(k, carry, reach=reach, width=width, lanes=lanes, rows=rows, row_lanes=row_lanes):
            matrix = out_ref[:reach, :]
            row = out_ref[pl.ds(k, 1), :]
            pivot = jnp.sum(jnp.where(row_lanes == k, row, 0.0), axis=1, keepdims=True)
            here = lanes == k
            col = jnp.sum(jnp.where(here, matrix, 0.0), axis=1, keepdims=True)
            recip = 1.0 / pivot
            scaled = jnp.where(row_lanes == k, recip, row * recip)
            out_ref[:reach, :] = jnp.where(here, 0.0, matrix) - jnp.where(rows == k, 0.0, col) * scaled
            out_ref[pl.ds(k, 1), :] = scaled
            return carry

        lax.fori_loop(start, min(size, start + segment), step, 0)


BLOCK = 32


def fold(value):
    half = value + pltpu.roll(value, 2 * BLOCK, 1)
    return half + pltpu.roll(half, BLOCK, 1)


def split_dot(exact, value, contract):
    total = None
    for _ in range(3):
        part = value.astype(jnp.bfloat16)
        value = value - part.astype(F32)
        term = lax.dot_general(*((exact, part) if contract[2] else (part, exact)), (contract[:2], ((), ())), preferred_element_type=F32)
        total = term if total is None else total + term
    return total


def pack(hot_ref, sums, dots=()):
    out = None
    for b in (0, 1):
        term = lax.dot_general(hot_ref[b], sums[b], (((1,), (1,)), ((), ())), precision=precise, preferred_element_type=F32)
        out = term if out is None else out + term
    if dots:
        sub = lax.broadcasted_iota(jnp.int32, out.shape, 0)
        ends = jnp.concatenate(list(dots), axis=0)
        full = sums[0].shape[0]
        if ends.shape[0] < full:
            ends = jnp.concatenate([ends, jnp.zeros((full - ends.shape[0], ends.shape[1]), F32)], axis=0)
        total = lax.dot_general(jnp.ones(out.shape[:1] + ends.shape[1:], F32), ends, (((1,), (1,)), ((), ())), precision=precise, preferred_element_type=F32)
        out = jnp.where(sub == out.shape[0] - 1, total, out)
    return out


def unpack(place_ref, gathered):
    block = lax.broadcasted_iota(jnp.int32, gathered.shape, 1) // BLOCK
    stacked = jnp.concatenate([jnp.where(block == k, gathered, 0.0) for k in range(4)], axis=0)
    return fold(split_dot(place_ref[...], stacked, ((1,), (0,), True)))


def gather_kernel(rows, cols, x_ref, out_ref, send_sem, recv_sem):
    count = rows * cols
    me = lax.axis_index("row") * cols + lax.axis_index("col")
    barrier = pltpu.get_barrier_semaphore()

    def target(d):
        other = lax.rem(me + d, count)
        return (other // cols, lax.rem(other, cols))

    def greet(d, carry):
        pl.semaphore_signal(barrier, inc=1, device_id=target(d), device_id_type=pl.DeviceIdType.MESH)
        return carry

    lax.fori_loop(1, count, greet, 0)
    pl.semaphore_wait(barrier, count - 1)

    def copy(d):
        return pltpu.make_async_remote_copy(
            src_ref=x_ref,
            dst_ref=out_ref.at[me],
            send_sem=send_sem.at[d],
            recv_sem=recv_sem.at[d],
            device_id=target(d),
            device_id_type=pl.DeviceIdType.MESH,
        )

    def send(d, carry):
        copy(d).start()
        return carry

    def finish(d, carry):
        copy(d).wait()
        return carry

    lax.fori_loop(1, count, send, 0)
    out_ref[pl.ds(me, 1)] = x_ref[...][None]
    lax.fori_loop(1, count, finish, 0)


def gather(value, ident):
    rows, cols = lax.axis_size("row"), lax.axis_size("col")
    count = rows * cols
    return pl.pallas_call(
        functools.partial(gather_kernel, rows, cols),
        out_shape=shape(count, *value.shape),
        in_specs=[VM],
        out_specs=VM,
        scratch_shapes=[pltpu.SemaphoreType.DMA((count,)), pltpu.SemaphoreType.DMA((count,))],
        compiler_params=pltpu.CompilerParams(collective_id=ident, has_side_effects=True),
    )(value)


def exchange_kernel(rows, cols, x_ref, out_ref, send_sem, recv_sem):
    r, c = lax.axis_index("row"), lax.axis_index("col")
    targets = (
        (lax.rem(r + 1, rows), c),
        (lax.rem(r + rows - 1, rows), c),
        (r, lax.rem(c + 1, cols)),
        (r, lax.rem(c + cols - 1, cols)),
    )
    barrier = pltpu.get_barrier_semaphore()
    for target in targets:
        pl.semaphore_signal(barrier, inc=1, device_id=target, device_id_type=pl.DeviceIdType.MESH)
    pl.semaphore_wait(barrier, 4)
    copies = [
        pltpu.make_async_remote_copy(
            src_ref=x_ref.at[k],
            dst_ref=out_ref.at[k],
            send_sem=send_sem.at[k],
            recv_sem=recv_sem.at[k],
            device_id=targets[k],
            device_id_type=pl.DeviceIdType.MESH,
        )
        for k in range(4)
    ]
    for copy in copies:
        copy.start()
    for copy in copies:
        copy.wait()


def exchange(value, ident):
    return pl.pallas_call(
        functools.partial(exchange_kernel, lax.axis_size("row"), lax.axis_size("col")),
        out_shape=shape(*value.shape),
        in_specs=[VM],
        out_specs=VM,
        scratch_shapes=[pltpu.SemaphoreType.DMA((4,)), pltpu.SemaphoreType.DMA((4,))],
        compiler_params=pltpu.CompilerParams(collective_id=ident, has_side_effects=True),
    )(value)


def matrix_kernel(plan, gathered_ref, place_ref, out_ref):
    diagonals = unpack(place_ref, gathered_ref[...])
    size = out_ref.shape[0]
    gap = lax.broadcasted_iota(jnp.int32, (size, size), 1) - lax.broadcasted_iota(jnp.int32, (size, size), 0)
    total = jnp.zeros((size, size), F32)
    for k in range(9):
        total = jnp.where(gap == REG * (k // 3 - 1) + k % 3 - 1, diagonals[:, k : k + 1], total)
    out_ref[...] = total
    sweep(size, out_ref)


def coarse_of(gathered, place_ref, inverse_ref):
    sums = unpack(place_ref, gathered)
    coarse = jnp.dot(inverse_ref[...], sums, precision=precise, preferred_element_type=F32)
    return sums, coarse


def expand_into(out_ref, coarse, expand_ref):
    near = split_dot(expand_ref[...], coarse, ((0,), (0,), False))
    loads = BLOCK
    cols = out_ref.shape[-1]
    levels = out_ref.shape[1] // loads
    for b in (0, 1):
        for l in range(levels):
            k = b * levels + l
            out_ref[b, l * loads : (l + 1) * loads, :] = near[:loads, k * cols : (k + 1) * cols]


def wide(value):
    return jnp.broadcast_to(value, (value.shape[1],) * 2).T[:BLOCK]


def totals(gathered_ref, count):
    summed = jnp.sum(gathered_ref[...].reshape(-1, 8, gathered_ref.shape[-1]), axis=0)[7:8]
    block = lax.broadcasted_iota(jnp.int32, summed.shape, 1) // BLOCK
    return [fold(jnp.where(block == k, summed, 0.0)) for k in range(count)]


def solve_first(plan, gathered_ref, place_ref, inverse_ref, expand_ref, cx_ref, c_ref):
    _, coarse = coarse_of(gathered_ref[...], place_ref, inverse_ref)
    c_ref[...] = coarse
    expand_into(cx_ref, coarse, expand_ref)


def solve_second(plan, gathered_ref, place_ref, inverse_ref, expand_ref, cx_ref, c_ref, scal_ref, alpha_ref):
    sums, coarse = coarse_of(gathered_ref[...], place_ref, inverse_ref)
    rho, image_dot = totals(gathered_ref, 2)
    curve = image_dot - jnp.sum(coarse * sums, axis=0, keepdims=True)
    alpha = rho / curve
    c_ref[...] = coarse
    scal_ref[0:1] = rho
    scal_ref[1:2] = curve
    scal_ref[2:3] = alpha
    alpha_ref[...] = wide(alpha)
    expand_into(cx_ref, coarse, expand_ref)


def solve_third(plan, gathered_ref, place_ref, inverse_ref, expand_ref, c0_ref, c1_ref, scal_ref, cs_ref, cx_ref, out_ref):
    sums, coarse = coarse_of(gathered_ref[...], place_ref, inverse_ref)
    rho1, qz, image_dot = totals(gathered_ref, 3)
    rho, curve, alpha0 = scal_ref[0:1], scal_ref[1:2], scal_ref[2:3]
    beta = rho1 / rho
    curve1 = image_dot - jnp.sum(coarse * sums, axis=0, keepdims=True) + 2.0 * beta * qz + beta * beta * curve
    alpha1 = rho1 / curve1
    mix = alpha0 + alpha1 * beta
    expand_into(cx_ref, coarse, expand_ref)
    expand_into(cs_ref, c0_ref[...] - alpha1 * coarse - mix * c1_ref[...], expand_ref)
    out_ref[0] = wide(mix)
    out_ref[1] = wide(alpha1)
    out_ref[2] = wide(beta)


class Plan:
    def __init__(self, rows, loads, height):
        self.rows, self.loads, self.height = rows, loads, height
        self.parts = rows // height + 1
        self.levels = self.parts + 1

    def chunks(self):
        half = self.height // 2
        for part in range(self.parts):
            yield part, max(0, part * self.height - half), min(self.rows, part * self.height + half)


def over_rows(first, last, step, init, group=4):
    def body(g, carry):
        for u in range(group):
            carry = step(first + g * group + u, carry)
        return carry

    return lax.fori_loop(0, (last - first) // group, body, init)


def row_of(ref, k, i):
    return ref[k, pl.ds(i, 1), :]


def spread(mask_ref, cx, i):
    out = row_of(mask_ref, 0, i) * cx[0]
    for k in range(1, 4):
        out = out + row_of(mask_ref, k, i) * cx[k]
    return out


def expansions(plan, cx_ref, part):
    n = plan.loads
    return [cx_ref[b, (part + a) * n : (part + a + 1) * n, :] for a in (0, 1) for b in (0, 1)]


def looked_up(table_ref, classes):
    out = jnp.zeros(classes.shape, F32)
    for k in range(table_ref.shape[0]):
        out = jnp.where(classes == k, table_ref[k], out)
    return out


def links_kernel(plan, h_ref, v_ref, label_ref, bump_ref, table_ref, link_ref, edge_ref):
    rows, cols = h_ref.shape
    last_row = lax.axis_index("row") == lax.axis_size("row") - 1
    last_col = lax.axis_index("col") == lax.axis_size("col") - 1
    i = lax.broadcasted_iota(jnp.int32, (rows, cols), 0)
    j = lax.broadcasted_iota(jnp.int32, (rows, cols), 1)
    row_end = jnp.where(last_row, rows - 1, rows)
    col_end = jnp.where(last_col, cols - 1, cols)
    right = jnp.where(j == col_end, 0.0, looked_up(table_ref, h_ref[...]))
    down = jnp.where(i == row_end, 0.0, looked_up(table_ref, v_ref[...]))
    link_ref[0] = right
    link_ref[1] = down
    edge_ref[...] = jnp.zeros_like(edge_ref)
    named = label_ref[...].astype(F32)
    bump = bump_ref[...]
    for k, value in enumerate((named, bump, down)):
        edge_ref[0, k : k + 1, :] = value[rows - 1 :]
        edge_ref[1, k : k + 1, :] = value[:1]
    for k, value in enumerate((named, bump, right)):
        turned = value.T
        edge_ref[2, k : k + 1, :] = turned[cols - 1 :]
        edge_ref[3, k : k + 1, :] = turned[:1]


def masks_kernel(plan, width, link_ref, edge_ref, label_ref, bump_ref, pad_ref, table_ref, mask_ref, image_ref, coef_ref):
    rows, cols = label_ref.shape
    i = lax.broadcasted_iota(jnp.int32, (rows, cols), 0)
    j = lax.broadcasted_iota(jnp.int32, (rows, cols), 1)

    def at_left(value, k):
        return jnp.where(j == 0, jnp.broadcast_to(edge_ref[2, k : k + 1, :], (cols, rows)).T, pltpu.roll(value, 1, 1))

    def at_right(value, k):
        return jnp.where(j == cols - 1, jnp.broadcast_to(edge_ref[3, k : k + 1, :], (cols, rows)).T, pltpu.roll(value, cols - 1, 1))

    def at_top(value, k):
        return jnp.where(i == 0, edge_ref[0, k : k + 1, :], pltpu.roll(value, 1, 0))

    def at_low(value, k):
        return jnp.where(i == rows - 1, edge_ref[1, k : k + 1, :], pltpu.roll(value, rows - 1, 0))

    right, down = link_ref[0], link_ref[1]
    left, upper = at_left(right, 2), at_top(down, 2)
    diagonal = looked_up(table_ref, pad_ref[...]) + right + left + down + upper
    for k, value in enumerate((diagonal, right, left, down, upper)):
        coef_ref[k] = value
    tile_row = (lax.axis_index("row") * (rows // plan.height) - 1).astype(F32)
    tile_col = (lax.axis_index("col") * (cols // width) - 1).astype(F32)
    base_row = jnp.zeros((rows, cols), F32) + tile_row
    base_col = jnp.zeros((rows, cols), F32) + tile_col
    for p in range(1, plan.parts):
        base_row = base_row + jnp.where(i >= p * plan.height - plan.height // 2, 1.0, 0.0)
    for p in range(1, cols // width + 1):
        base_col = base_col + jnp.where(j >= p * width - width // 2, 1.0, 0.0)
    named, bump = label_ref[...].astype(F32), bump_ref[...]
    total = None
    for label, weight in (
        (named, diagonal * bump),
        (at_right(named, 0), -right * at_right(bump, 1)),
        (at_left(named, 0), -left * at_left(bump, 1)),
        (at_low(named, 0), -down * at_low(bump, 1)),
        (at_top(named, 0), -upper * at_top(bump, 1)),
    ):
        high = jnp.floor(label * (1.0 / REG))
        a, b = high - base_row, label - REG * high - base_col
        hits = [(a == m) & (b == n) for m in (0.0, 1.0) for n in (0.0, 1.0)]
        if total is None:
            for k in range(4):
                mask_ref[k] = jnp.where(hits[k], bump, 0.0)
        terms = [jnp.where(hit, weight, 0.0) for hit in hits]
        total = terms if total is None else [t + u for t, u in zip(total, terms)]
    for k in range(4):
        image_ref[k] = total[k]


def sums_kernel(plan, b_ref, mask_ref, image_ref, hot_ref, out_ref, s_ref, pair_ref):
    n = plan.loads
    s_ref[...] = jnp.zeros_like(s_ref)
    for part, first, last in plan.chunks():
        def step(i, acc):
            v = b_ref[pl.ds(i, n, stride=plan.rows), :]
            return tuple(x + row_of(mask_ref, k, i) * v for k, x in enumerate(acc))

        acc = over_rows(first, last, step, (jnp.zeros((n, s_ref.shape[-1]), F32),) * 4)
        add_sums(plan, s_ref, part, acc)
    out_ref[0] = pack(hot_ref, s_ref)
    pair_ref[...] = jnp.zeros_like(pair_ref)
    for part, first, last in plan.chunks():
        for k in range(4):
            for m in range(4):
                da, db = m // 2 - k // 2, m % 2 - k % 2
                at = (part + k // 2) * BLOCK + (da + 1) * 3 + db + 1
                term = jnp.sum(mask_ref[k, first:last, :] * image_ref[m, first:last, :], axis=0, keepdims=True)
                pair_ref[k % 2, at : at + 1, :] = pair_ref[k % 2, at : at + 1, :] + term
    out_ref[1] = pack(hot_ref, pair_ref)


def add_sums(plan, s_ref, part, acc):
    n = plan.loads
    for a in (0, 1):
        for b in (0, 1):
            where = slice((part + a) * n, (part + a + 1) * n)
            s_ref[b, where, :] = s_ref[b, where, :] + acc[2 * a + b]


def pack_edges(edges, z, i, cols):
    left, right = edges
    lane = lax.broadcasted_iota(jnp.int32, z.shape, 1)
    left = jnp.where(lane == i, pltpu.roll(z, i, 1), left)
    right = jnp.where(lane == i, pltpu.roll(z, lax.rem(i + 1, z.shape[1]), 1), right)
    return left, right


def first_kernel(plan, b_ref, image_ref, coef_ref, cx_ref, r_ref, z_ref, rho_ref, edge_ref):
    n = plan.loads
    zero = jnp.zeros((n, b_ref.shape[-1]), F32)
    carry = (zero, zero, zero)
    for part, first, last in plan.chunks():
        cx = expansions(plan, cx_ref, part)

        def step(i, carry):
            rho, *edges = carry
            r = b_ref[pl.ds(i, n, stride=plan.rows), :] - spread(image_ref, cx, i)
            z = r / row_of(coef_ref, 0, i)
            at = pl.ds(pl.multiple_of(i * n, n), n)
            r_ref[at, :] = r
            z_ref[at, :] = z
            return (rho + r * z, *pack_edges(edges, z, i, z.shape[1]))

        carry = over_rows(first, last, step, carry)
    rho_ref[0] = carry[0]
    edge_ref[0] = z_ref[(plan.rows - 1) * n :, :]
    edge_ref[1] = z_ref[:n, :]
    edge_ref[2] = carry[2]
    edge_ref[3] = carry[1]


def image_kernel(plan, z_ref, edge_ref, coef_ref, mask_ref, hot_ref, dots_ref, f_ref, out_ref, s_ref):
    n = plan.loads
    cols = z_ref.shape[-1]
    zero = jnp.zeros((n, cols), F32)
    lane = lax.broadcasted_iota(jnp.int32, (n, cols), 1)
    s_ref[...] = jnp.zeros_like(s_ref)
    left_pack, right_pack = edge_ref[2], edge_ref[3]

    def image(i, z, up, down):
        before = jnp.where(lane == 0, pltpu.roll(left_pack, lax.rem(cols - i, cols), 1), pltpu.roll(z, 1, 1))
        after = jnp.where(lane == cols - 1, pltpu.roll(right_pack, cols - 1 - i, 1), pltpu.roll(z, cols - 1, 1))
        return (
            row_of(coef_ref, 0, i) * z
            - row_of(coef_ref, 1, i) * after
            - row_of(coef_ref, 2, i) * before
            - row_of(coef_ref, 3, i) * down
            - row_of(coef_ref, 4, i) * up
        )

    def load(i):
        return z_ref[pl.ds(pl.multiple_of(i * n, n), n), :]

    def step(i, carry):
        return finish(i, load(i), load(i - 1), load(i + 1), carry)

    def finish(i, z, up, down, carry):
        f = image(i, z, up, down)
        f_ref[pl.ds(pl.multiple_of(i * n, n), n), :] = f
        zf, *acc = carry
        return (zf + z * f, *[x + row_of(mask_ref, k, i) * f for k, x in enumerate(acc)])

    zf = zero
    for part, first, last in plan.chunks():
        carry = (zf,) + (zero,) * 4
        low, high = first, last
        if first == 0:
            carry = finish(0, load(0), edge_ref[0], load(1), carry)
            low = 1
        if last == plan.rows:
            high = last - 1
        while (high - low) % 4:
            carry = step(low, carry)
            low += 1
        carry = over_rows(low, high, step, carry)
        if last == plan.rows:
            carry = finish(last - 1, load(last - 1), load(last - 2), edge_ref[1], carry)
        zf, *acc = carry
        add_sums(plan, s_ref, part, acc)
    out_ref[...] = pack(hot_ref, s_ref, [dots_ref[k] for k in range(dots_ref.shape[0])] + [zf])


def second_kernel(plan, r_ref, f_ref, image_ref, coef_ref, cx_ref, alpha_ref, r1_ref, z1_ref, q_ref, dots_ref, edge_ref):
    n = plan.loads
    zero = jnp.zeros((n, r_ref.shape[-1]), F32)
    carry = (zero,) * 4
    alpha = alpha_ref[...]
    for part, first, last in plan.chunks():
        cx = expansions(plan, cx_ref, part)

        def step(i, carry):
            rho, qz, *edges = carry
            at = pl.ds(pl.multiple_of(i * n, n), n)
            q = f_ref[at, :] - spread(image_ref, cx, i)
            r = r_ref[at, :] - alpha * q
            z = r / row_of(coef_ref, 0, i)
            q_ref[at, :] = q
            r1_ref[at, :] = r
            z1_ref[at, :] = z
            return (rho + r * z, qz + q * z, *pack_edges(edges, z, i, z.shape[1]))

        carry = over_rows(first, last, step, carry)
    dots_ref[0] = carry[0]
    dots_ref[1] = carry[1]
    edge_ref[0] = z1_ref[(plan.rows - 1) * n :, :]
    edge_ref[1] = z1_ref[:n, :]
    edge_ref[2] = carry[3]
    edge_ref[3] = carry[2]


def last_kernel(plan, z_ref, z1_ref, r1_ref, f1_ref, q_ref, mask_ref, image_ref, cs_ref, cx_ref, scal_ref, s_out, r_out):
    n = plan.loads
    mix, alpha, beta = scal_ref[0], scal_ref[1], scal_ref[2]
    for part, first, last in plan.chunks():
        cs = expansions(plan, cs_ref, part)
        cx = expansions(plan, cx_ref, part)

        def step(i, carry):
            at = pl.ds(pl.multiple_of(i * n, n), n)
            to = pl.ds(i, n, stride=plan.rows)
            s_out[to, :] = spread(mask_ref, cs, i) + mix * z_ref[at, :] + alpha * z1_ref[at, :]
            q1 = f1_ref[at, :] - spread(image_ref, cx, i) + beta * q_ref[at, :]
            r_out[to, :] = r1_ref[at, :] - alpha * q1
            return carry

        over_rows(first, last, step, 0, 2)


def body(load_currents, labels, bump_height, horizontal_class, vertical_class, pad_class, edge_table, pad_table):
    rows, cols = labels.shape
    loads = load_currents.shape[0]
    regions = REG * REG
    grid_rows = lax.axis_size("row") * rows
    grid_cols = lax.axis_size("col") * cols
    height, width = grid_rows // REG, grid_cols // REG
    plan = Plan(rows, loads, height)
    levels = plan.levels
    ri, ci = lax.axis_index("row"), lax.axis_index("col")
    smem = pl.BlockSpec(memory_space=pltpu.SMEM)
    links, ends = pl.pallas_call(
        functools.partial(links_kernel, plan),
        out_shape=(shape(2, rows, cols), shape(4, 8, cols)),
        in_specs=[VM] * 4 + [smem],
        out_specs=(VM, VM),
        compiler_params=PARAMS,
    )(horizontal_class, vertical_class, labels, bump_height, edge_table)
    ends = exchange(ends, 5)
    mask, image, coef = pl.pallas_call(
        functools.partial(masks_kernel, plan, width),
        out_shape=(shape(4, rows, cols), shape(4, rows, cols), shape(5, rows, cols)),
        in_specs=[VM] * 5 + [smem],
        out_specs=(VM,) * 3,
        compiler_params=PARAMS,
    )(links, ends, labels, bump_height, pad_class, pad_table)

    span = cols // width + 2
    lane_base = (lax.iota(jnp.int32, cols) + width // 2) // width
    hot = jnp.stack([(lane_base[None] + b == lax.iota(jnp.int32, 8)[:, None]).astype(F32) for b in (0, 1)])
    count = lax.axis_size("row") * lax.axis_size("col")
    here = lax.broadcasted_iota(jnp.int32, (regions, 4 * count * 8), 0)
    sent = lax.broadcasted_iota(jnp.int32, (regions, 4 * count * 8), 1)
    level, device, x = sent // (count * 8), sent // 8 % count, sent % 8
    at_row = device // lax.axis_size("col") * (rows // height) - 1 + level
    at_col = device % lax.axis_size("col") * (cols // width) - 1 + x
    place = ((here // REG == at_row) & (here % REG == at_col) & (x < span) & (level < levels)).astype(jnp.bfloat16)
    here = lax.broadcasted_iota(jnp.int32, (regions, 2 * levels * cols), 0)
    lane = lax.broadcasted_iota(jnp.int32, (regions, 2 * levels * cols), 1)
    which, lane = lane // cols, lane % cols
    at_row = ri * (rows // height) - 1 + which % levels
    at_col = ci * (cols // width) - 1 + (lane + width // 2) // width + which // levels
    expand = ((here // REG == at_row) & (here % REG == at_col)).astype(jnp.bfloat16)

    def call(kernel, outs, *args, scratch=()):
        return pl.pallas_call(
            functools.partial(kernel, plan),
            out_shape=outs,
            in_specs=[VM] * len(args),
            out_specs=jax.tree.map(lambda _: VM, outs),
            scratch_shapes=scratch,
            compiler_params=PARAMS,
        )(*args)

    s_shape = shape(2, levels * loads, cols)
    sums_scratch = [pltpu.VMEM((2, 4 * BLOCK, cols), F32)]
    field = shape(rows * loads, cols)
    message = shape(8, 4 * BLOCK)
    coarse_shape = shape(regions, 4 * BLOCK)

    def image_of(z, edges, dots, ident):
        landed = exchange(edges, ident)
        f, sums = call(image_kernel, (field, message), z, landed, coef, mask, hot, dots, scratch=sums_scratch)
        return f, gather(sums, ident + 1).reshape(count * 8, 4 * BLOCK)

    flat = load_currents.reshape(loads * rows, cols)
    first = call(sums_kernel, shape(2, 8, 4 * BLOCK), flat, mask, image, hot, scratch=sums_scratch * 2)
    first = gather(first, 0)
    inverse = call(matrix_kernel, shape(regions, regions), first[:, 1].reshape(count * 8, 4 * BLOCK), place)
    cx, c0 = call(solve_first, (s_shape, coarse_shape), first[:, 0].reshape(count * 8, 4 * BLOCK), place, inverse, expand)
    r0, z0, rho_lanes, edges = call(
        first_kernel, (field, field, shape(1, loads, cols), shape(4, loads, cols)), flat, image, coef, cx
    )
    f0, sums = image_of(z0, edges, rho_lanes, 1)
    cx, c1, scal, alpha = call(
        solve_second, (s_shape, coarse_shape, shape(8, 4 * BLOCK), shape(loads, cols)), sums, place, inverse, expand
    )
    r1, z1, q0, dots, edges = call(
        second_kernel,
        (field, field, field, shape(2, loads, cols), shape(4, loads, cols)),
        r0, f0, image, coef, cx, alpha,
    )
    f1, sums = image_of(z1, edges, dots, 3)
    cs, cx, scal = call(
        solve_third, (s_shape, s_shape, shape(3, loads, cols)), sums, place, inverse, expand, c0, c1, scal
    )
    s, r = call(
        last_kernel, (shape(loads * rows, cols),) * 2,
        z0, z1, r1, f1, q0, mask, image, cs, cx, scal,
    )
    return (s.reshape(load_currents.shape), r.reshape(load_currents.shape))


def solution(mesh):
    grid = P("row", "col")
    cube = P(None, "row", "col")
    return jax.shard_map(
        body,
        mesh=mesh,
        in_specs=(cube, grid, grid, grid, grid, grid, P(), P()),
        out_specs=(cube, cube),
        check_vma=False,
    )
```

profile of v0, /device:TPU:0, one launch (start us, length us, event | category | flops | bytes accessed | tf_op | source)
XLA Modules:
  0.0 161.8 jit_solution(11233528058185332982)
XLA Ops:
  0.8 0.6 add_convert_fusion.hot_ref
  1.4 1.7 %shard_map.95 = (f32[2,128,128]{2,1,0:T(8,128)}, f32[4,8,128]{2,1,0:T(8,128)}) custom-call(s32[128,128]{1,0:T(8,128)} %h_ref.1, s32[128,128]{1,0:T(8,128)} %v_ref.1, s32[128,128]{1,0:T(8,128)} %label_ref.3, f32[128,128]{1,0:T(8,128)} %bump_ref.3, f32[8]{0:T(128)} %table_ref.2), custom_call_target="tpu_custom_call" | custom-call | tf_op jit(solution)/shard_map/pallas_call | solution.py:538
  3.1 10.0 %shard_map.96.edge_ref = f32[4,8,128]{2,1,0:T(8,128)} custom-call(f32[4,8,128]{2,1,0:T(8,128)} %get-tuple-element.32.x_ref), custom_call_target="tpu_custom_call" | custom-call | tf_op jit(solution)/shard_map/pallas_call | solution.py:167
  13.1 1.3 fusion.19.place_ref
  14.4 1.2 fusion.16.expand_ref
  15.5 2.2 %shard_map.97 = (f32[4,128,128]{2,1,0:T(8,128)}, f32[4,128,128]{2,1,0:T(8,128)}, f32[5,128,128]{2,1,0:T(8,128)}) custom-call(f32[2,128,128]{2,1,0:T(8,128)} %get-tuple-element.31.link_ref, f32[4,8,128]{2,1,0:T(8,128)} %shard_map.96.edge_ref, s32[128,128]{1,0:T(8,128)} %label_ref.3, f32[128,128]{1,0:T(8,128)} %bump_ref.3, s32[128,128]{1,0:T(8,128)} %pad_ref.1, ...), custom_call_target="tpu_custom_call" | custom-call | tf_op jit(solution)/shard_map/pallas_call | solution.py:546
  17.8 4.5 %shard_map.98.x_ref = f32[2,8,128]{2,1,0:T(8,128)} custom-call(f32[4096,128]{1,0:T(8,128)} %bitcast.9, f32[4,128,128]{2,1,0:T(8,128)} %get-tuple-element.35.mask_ref, f32[4,128,128]{2,1,0:T(8,128)} %get-tuple-element.33.image_ref, f32[2,8,128]{2,1,0:T(8,128)} %add_convert_fusion.hot_ref), custom_call_target="tpu_custom_call" | custom-call | tf_op jit(solution)/shard_map/pallas_call | solution.py:572
  22.3 11.7 %shard_map.99 = f32[32,2,8,128]{3,2,1,0:T(8,128)} custom-call(f32[2,8,128]{2,1,0:T(8,128)} %shard_map.98.x_ref), custom_call_target="tpu_custom_call" | custom-call | tf_op jit(solution)/shard_map/pallas_call | solution.py:127
  34.0 1.7 %slice_bitcast_fusion = (f32[256,128]{1,0:T(8,128)}, f32[256,128]{1,0:T(8,128)}) fusion(f32[32,2,8,128]{3,2,1,0:T(8,128)} %shard_map.99), kind=kLoop, calls=%fused_computation.54 | loop fusion | bytes 524288 | tf_op jit(solution)/shard_map/reshape;squeeze | solution.py:595
  35.7 33.0 %shard_map.100.inverse_ref = f32[256,256]{1,0:T(8,128)} custom-call(f32[256,128]{1,0:T(8,128)} %get-tuple-element.60.gathered_ref, bf16[256,1024]{1,0:T(8,128)(2,1)} %fusion.19.place_ref), custom_call_target="tpu_custom_call" | custom-call | tf_op jit(solution)/shard_map/pallas_call | solution.py:572
  68.7 3.8 %shard_map.101 = (f32[2,128,128]{2,1,0:T(8,128)}, f32[256,128]{1,0:T(8,128)}) custom-call(f32[256,128]{1,0:T(8,128)} %get-tuple-element.61.gathered_ref, bf16[256,1024]{1,0:T(8,128)(2,1)} %fusion.19.place_ref, f32[256,256]{1,0:T(8,128)} %shard_map.100.inverse_ref, bf16[256,1024]{1,0:T(8,128)(2,1)} %fusion.16.expand_ref), custom_call_target="tpu_custom_call" | custom-call | tf_op jit(solution)/shard_map/pallas_call | solution.py:572
  72.5 8.0 %shard_map.102 = (f32[4096,128]{1,0:T(8,128)}, f32[4096,128]{1,0:T(8,128)}, f32[1,32,128]{2,1,0:T(8,128)}, f32[4,32,128]{2,1,0:T(8,128)}) custom-call(f32[4096,128]{1,0:T(8,128)} %bitcast.10, f32[4,128,128]{2,1,0:T(8,128)} %get-tuple-element.33.image_ref, f32[5,128,128]{2,1,0:T(8,128)} %get-tuple-element.34.coef_ref, f32[2,128,128]{2,1,0:T(8,128)} %get-tuple-element.36.cx_ref), custom_call_target="tpu_custom_call" | custom-call | tf_op jit(solution)/shard_map/pallas_call | solution.py:572
  80.4 9.8 %shard_map.103.edge_ref = f32[4,32,128]{2,1,0:T(8,128)} custom-call(f32[4,32,128]{2,1,0:T(8,128)} %get-tuple-element.39.x_ref), custom_call_target="tpu_custom_call" | custom-call | tf_op jit(solution)/shard_map/pallas_call | solution.py:167
  90.2 7.9 %shard_map.104 = (f32[4096,128]{1,0:T(8,128)}, f32[8,128]{1,0:T(8,128)}) custom-call(f32[4096,128]{1,0:T(8,128)} %get-tuple-element.37.z_ref, f32[4,32,128]{2,1,0:T(8,128)} %shard_map.103.edge_ref, f32[5,128,128]{2,1,0:T(8,128)} %get-tuple-element.34.coef_ref, f32[4,128,128]{2,1,0:T(8,128)} %get-tuple-element.35.mask_ref, ...), custom_call_target="tpu_custom_call" | custom-call | tf_op jit(solution)/shard_map/pallas_call | solution.py:572
  98.1 9.7 %shard_map.105 = f32[32,8,128]{2,1,0:T(8,128)} custom-call(f32[8,128]{1,0:T(8,128)} %get-tuple-element.42.x_ref), custom_call_target="tpu_custom_call" | custom-call | tf_op jit(solution)/shard_map/pallas_call | solution.py:127
  107.8 3.8 %shard_map.106 = (f32[2,128,128]{2,1,0:T(8,128)}, f32[256,128]{1,0:T(8,128)}, f32[8,128]{1,0:T(8,128)}, f32[32,128]{1,0:T(8,128)}) custom-call(f32[256,128]{1,0:T(8,128)} %bitcast.12, bf16[256,1024]{1,0:T(8,128)(2,1)} %fusion.19.place_ref, f32[256,256]{1,0:T(8,128)} %shard_map.100.inverse_ref, bf16[256,1024]{1,0:T(8,128)(2,1)} %fusion.16.expand_ref), custom_call_target="tpu_custom_call" | custom-call | tf_op jit(solution)/shard_map/pallas_call | solution.py:572
  111.5 8.6 %shard_map.107 = (f32[4096,128]{1,0:T(8,128)}, f32[4096,128]{1,0:T(8,128)}, f32[4096,128]{1,0:T(8,128)}, f32[2,32,128]{2,1,0:T(8,128)}, f32[4,32,128]{2,1,0:T(8,128)}) custom-call(f32[4096,128]{1,0:T(8,128)} %get-tuple-element.38.r_ref, f32[4096,128]{1,0:T(8,128)} %get-tuple-element.41.f_ref, f32[4,128,128]{2,1,0:T(8,128)} %get-tuple-element.33.image_ref, ...), custom_call_target="tpu_custom_call" | custom-call | tf_op jit(solution)/shard_map/pallas_call | solution.py:572
  120.1 8.8 %shard_map.108.edge_ref = f32[4,32,128]{2,1,0:T(8,128)} custom-call(f32[4,32,128]{2,1,0:T(8,128)} %get-tuple-element.47.x_ref), custom_call_target="tpu_custom_call" | custom-call | tf_op jit(solution)/shard_map/pallas_call | solution.py:167
  129.0 8.0 %shard_map.109 = (f32[4096,128]{1,0:T(8,128)}, f32[8,128]{1,0:T(8,128)}) custom-call(f32[4096,128]{1,0:T(8,128)} %get-tuple-element.45.z_ref.z1_ref, f32[4,32,128]{2,1,0:T(8,128)} %shard_map.108.edge_ref, f32[5,128,128]{2,1,0:T(8,128)} %get-tuple-element.34.coef_ref, f32[4,128,128]{2,1,0:T(8,128)} %get-tuple-element.35.mask_ref, ...), custom_call_target="tpu_custom_call" | custom-call | tf_op jit(solution)/shard_map/pallas_call | solution.py:572
  136.9 9.7 %shard_map.110 = f32[32,8,128]{2,1,0:T(8,128)} custom-call(f32[8,128]{1,0:T(8,128)} %get-tuple-element.51.x_ref), custom_call_target="tpu_custom_call" | custom-call | tf_op jit(solution)/shard_map/pallas_call | solution.py:127
  146.6 4.0 %shard_map.111 = (f32[2,128,128]{2,1,0:T(8,128)}, f32[2,128,128]{2,1,0:T(8,128)}, f32[3,32,128]{2,1,0:T(8,128)}) custom-call(f32[256,128]{1,0:T(8,128)} %bitcast.11, bf16[256,1024]{1,0:T(8,128)(2,1)} %fusion.19.place_ref, f32[256,256]{1,0:T(8,128)} %shard_map.100.inverse_ref, bf16[256,1024]{1,0:T(8,128)(2,1)} %fusion.16.expand_ref, ...), custom_call_target="tpu_custom_call" | custom-call | tf_op jit(solution)/shard_map/pallas_call | solution.py:572
  150.7 11.1 %shard_map.112 = (f32[4096,128]{1,0:T(8,128)}, f32[4096,128]{1,0:T(8,128)}) custom-call(f32[4096,128]{1,0:T(8,128)} %get-tuple-element.37.z_ref, f32[4096,128]{1,0:T(8,128)} %get-tuple-element.45.z_ref.z1_ref, f32[4096,128]{1,0:T(8,128)} %get-tuple-element.46.r1_ref, f32[4096,128]{1,0:T(8,128)} %get-tuple-element.49.f1_ref, ...), custom_call_target="tpu_custom_call" | custom-call | tf_op jit(solution)/shard_map/pallas_call | solution.py:572
  (14 shorter events, 0.1 us)
where the time goes:
time: 162 us
  Pallas kernels  156 us (96%)
  other arithmetic  3.12 us (2%)
  local copies, waits for them, and re-layouts  1.69 us (1%)
    pallas_call x10, Pallas kernels, call(): pl.pallas_call(functools.partial(kernel, plan), out_shape=outs, in_specs=...  92.7 us
    pallas_call x3, Pallas kernels, gather(): pl.pallas_call(functools.partial(gather_kernel, rows, cols), out_shape=sh...  31 us
    pallas_call x3, Pallas kernels, exchange(): pl.pallas_call(functools.partial(exchange_kernel, lax.axis_size('row'), l...  28.6 us

commit v1 on v0

v1 whole, which is shorter than its diff:
```python
import functools

import jax
import jax.numpy as jnp
from jax import lax
from jax.experimental import pallas as pl
from jax.experimental.pallas import tpu as pltpu
from jax.sharding import PartitionSpec as P

REG = 16
F32 = jnp.float32
precise = lax.Precision.HIGHEST
VM = pl.BlockSpec(memory_space=pltpu.VMEM)
SM = pl.BlockSpec(memory_space=pltpu.SMEM)
ANY = pl.BlockSpec(memory_space=pl.ANY)
BLOCK = 32
LANES = 4 * BLOCK
PITCH = 8
MINV, Z, W0, W1, W2, V0, V1, CO = 0, 1, 5, 9, 13, 17, 21, 25
KEPT, PLANES = 17, 30
ORDER = (0, 2, 4, 6, 8, 10, 12, 14, 1, 5, 9, 13, 3, 11, 7, 15)


def shape(*dims):
    return jax.ShapeDtypeStruct(dims, F32)


def iota(dims, axis):
    return lax.broadcasted_iota(jnp.int32, dims, axis)


def rolled(value, shift, axis):
    shift = shift % value.shape[axis]
    return pltpu.roll(value, shift, axis) if shift else value


class Plan:
    def __init__(self, rows, cols, loads, height, width, row_devices, col_devices):
        self.rows, self.cols, self.loads = rows, cols, loads
        self.height, self.width = height, width
        self.nr, self.nc = row_devices, col_devices
        self.count = row_devices * col_devices
        self.lv, self.cw = rows // height, cols // width
        self.parts = self.lv + 1
        self.levels = self.lv + 2
        self.half = loads // 2
        self.pitch = rows + PITCH

    def chunks(self):
        half = self.height // 2
        for part in range(self.parts):
            yield part, max(0, part * self.height - half), min(self.rows, part * self.height + half)


def over_rows(first, last, step, init, group=4):
    def body(g, carry):
        for u in range(group):
            carry = step(first + g * group + u, u, carry)
        return carry

    return lax.fori_loop(0, (last - first) // group, body, init)


def row_of(ref, k, i):
    return ref[k, pl.ds(i, 1), :]


class Legs:
    def __init__(self, plan, send_sem, recv_sem):
        self.plan, self.send_sem, self.recv_sem = plan, send_sem, recv_sem
        self.used = 0
        self.r, self.c = lax.axis_index("row"), lax.axis_index("col")
        self.everything = []

    def inside(self, dr, dc):
        r, c = self.r + dr, self.c + dc
        return (r >= 0) & (r < self.plan.nr) & (c >= 0) & (c < self.plan.nc)

    def make(self, items):
        out = []
        for dr, dc, src, dst in items:
            target = (lax.rem(self.r + dr + self.plan.nr, self.plan.nr), lax.rem(self.c + dc + self.plan.nc, self.plan.nc))
            copy = pltpu.make_async_remote_copy(
                src_ref=src,
                dst_ref=dst,
                send_sem=self.send_sem.at[self.used],
                recv_sem=self.recv_sem.at[self.used],
                device_id=target,
                device_id_type=pl.DeviceIdType.MESH,
            )
            self.used += 1
            out.append((self.inside(dr, dc), self.inside(-dr, -dc), copy))
        self.everything += out
        return out

    def start(self, legs):
        for goes, _, copy in legs:
            pl.when(goes)(copy.start)

    def wait(self, legs):
        for _, comes, copy in legs:
            pl.when(comes)(copy.wait_recv)

    def finish(self):
        for goes, _, copy in self.everything:
            pl.when(goes)(copy.wait_send)


def beside(src, dst):
    return [(1, 0, src.at[0], dst.at[0]), (-1, 0, src.at[1], dst.at[1]), (0, 1, src.at[2], dst.at[2]), (0, -1, src.at[3], dst.at[3])]


def looked_up(table_ref, classes):
    out = jnp.zeros(classes.shape, F32)
    for k in range(table_ref.shape[0]):
        out = jnp.where(classes == k, table_ref[k], out)
    return out


def put_edges(ref, k, value, row_end=True):
    rows, cols = value.shape
    ref[0, k : k + 1, :] = value[rows - 1 :]
    ref[1, k : k + 1, :] = value[:1]
    turned = value.T
    ref[2, k : k + 1, :] = turned[cols - 1 :]
    ref[3, k : k + 1, :] = turned[:1]


class Around:
    def __init__(self, edge_ref, rows, cols):
        self.edge_ref, self.rows, self.cols = edge_ref, rows, cols
        self.i, self.j = iota((rows, cols), 0), iota((rows, cols), 1)

    def column(self, side, k):
        return jnp.broadcast_to(self.edge_ref[side, k : k + 1, :], (self.cols, self.rows)).T

    def left(self, value, k):
        return jnp.where(self.j == 0, self.column(2, k), pltpu.roll(value, 1, 1))

    def right(self, value, k):
        return jnp.where(self.j == self.cols - 1, self.column(3, k), pltpu.roll(value, self.cols - 1, 1))

    def top(self, value, k):
        return jnp.where(self.i == 0, self.edge_ref[0, k : k + 1, :], pltpu.roll(value, 1, 0))

    def low(self, value, k):
        return jnp.where(self.i == self.rows - 1, self.edge_ref[1, k : k + 1, :], pltpu.roll(value, self.rows - 1, 0))

    def turns(self, at, size, step):
        out = None
        for p in range(1, size // step + 1):
            hit = at == p * step - step // 2
            out = hit if out is None else out | hit
        return out

    def images(self, plan, planes, source, k):
        values = [planes[source + m] for m in range(4)]
        to_right = self.turns(self.j + 1, plan.cols, plan.width)
        to_left = self.turns(self.j, plan.cols, plan.width)
        to_low = self.turns(self.i + 1, plan.rows, plan.height)
        to_top = self.turns(self.i, plan.rows, plan.height)

        def shifted(reader, turn, step, later):
            seen = [reader(value, k + m) for m, value in enumerate(values)]
            out = list(seen)
            for m in range(4):
                if bool(m & step) == later:
                    out[m] = jnp.where(turn, seen[m ^ step], seen[m])
                else:
                    out[m] = jnp.where(turn, 0.0, seen[m])
            return out

        right = shifted(self.right, to_right, 1, True)
        left = shifted(self.left, to_left, 1, False)
        low = shifted(self.low, to_low, 2, True)
        top = shifted(self.top, to_top, 2, False)
        return [
            planes[CO] * values[m]
            - planes[CO + 1] * right[m]
            - planes[CO + 2] * left[m]
            - planes[CO + 3] * low[m]
            - planes[CO + 4] * top[m]
            for m in range(4)
        ]


def windows(plan):
    rows, cols = plan.rows, plan.cols
    i, j = iota((rows, cols), 0), iota((rows, cols), 1)
    base_row = jnp.zeros((rows, cols), F32) + (lax.axis_index("row") * plan.lv - 1).astype(F32)
    base_col = jnp.zeros((rows, cols), F32) + (lax.axis_index("col") * plan.cw - 1).astype(F32)
    for p in range(1, plan.parts):
        base_row = base_row + jnp.where(i >= p * plan.height - plan.height // 2, 1.0, 0.0)
    for p in range(1, plan.cw + 1):
        base_col = base_col + jnp.where(j >= p * plan.width - plan.width // 2, 1.0, 0.0)
    return base_row, base_col


def hits_of(label, base_row, base_col):
    high = jnp.floor(label * (1.0 / REG))
    a, b = high - base_row, label - REG * high - base_col
    return [(a == m) & (b == n) for m in (0.0, 1.0) for n in (0.0, 1.0)]


def add_sums(plan, s_ref, h, part, acc):
    n, hn = plan.loads, plan.half
    for a in (0, 1):
        for b in (0, 1):
            at = (part + a) * n + h * hn
            s_ref[b, at : at + hn, :] = s_ref[b, at : at + hn, :] + acc[2 * a + b]


def packed(plan, s_ref):
    out = [None] * (plan.cw + 2)
    half = plan.width // 2
    for b in (0, 1):
        turned = s_ref[b].T
        for g in range(plan.cw + 1):
            part = turned[max(0, g * plan.width - half) : min(plan.cols, g * plan.width + half)]
            term = jnp.sum(part, axis=0, keepdims=True)
            out[g + b] = term if out[g + b] is None else out[g + b] + term
    out.append(jnp.zeros((8 - len(out), LANES), F32))
    return jnp.concatenate(out, axis=0)


def pair_sums(plan, planes, x, y, pair_ref, q):
    terms = {}
    for part, first, last in plan.chunks():
        for k in range(4):
            for m in range(4):
                da, db = m // 2 - k // 2, m % 2 - k % 2
                at = (k % 2, (part + k // 2) * BLOCK + q + (da + 1) * 3 + db + 1)
                term = jnp.sum(planes[x + k, first:last, :] * planes[y + m, first:last, :], axis=0, keepdims=True)
                terms[at] = term if at not in terms else terms[at] + term
    for (b, at), term in terms.items():
        pair_ref[b, at : at + 1, :] = term


class Spread:
    def __init__(self, plan, legs, planes, sides, got_planes, got_sides):
        self.plan, self.planes, self.sides = plan, planes, sides
        self.got_planes, self.got_sides = got_planes, got_sides
        west, east = sides.at[0], sides.at[1]
        self.legs = legs
        self.mine = legs.make([
            (1, 0, planes, got_planes.at[0]),
            (-1, 0, planes, got_planes.at[1]),
            (0, -1, west, got_sides.at[0]),
            (1, -1, west, got_sides.at[1]),
            (-1, -1, west, got_sides.at[2]),
            (0, 1, east, got_sides.at[3]),
            (1, 1, east, got_sides.at[4]),
            (-1, 1, east, got_sides.at[5]),
        ])

    def send(self, values):
        last = self.plan.cw + 1
        for k, value in enumerate(values):
            self.planes[k] = value
            self.sides[0, k : k + 1, :] = value[:1]
            self.sides[1, k : k + 1, :] = value[last : last + 1]
        self.legs.start(self.mine)

    def meet(self, own, above, below):
        lv = self.plan.lv
        block = iota(own.shape, len(own.shape) - 1) // BLOCK
        shift = lv * BLOCK
        return own + jnp.where(block == 1, rolled(above, -shift, 1), 0.0) + jnp.where(block == lv, rolled(below, shift, 1), 0.0)

    def merged(self):
        self.legs.wait(self.mine)
        sub = iota((8, LANES), 0)
        sides = self.got_sides
        right = self.meet(sides[0], sides[1], sides[2])
        left = self.meet(sides[3], sides[4], sides[5])
        out = []
        for k in range(self.planes.shape[0]):
            value = self.meet(self.planes[k], self.got_planes[0, k], self.got_planes[1, k])
            value = value + jnp.where(sub == self.plan.cw, right[k : k + 1], 0.0) + jnp.where(sub == 1, left[k : k + 1], 0.0)
            out.append(value)
        return out


def message(plan, pieces):
    sub, block = iota((8, LANES), 0), iota((8, LANES), 1) // BLOCK
    out = jnp.zeros((8, LANES), F32)
    for spot, value in pieces:
        for l in range(plan.lv):
            first = l * plan.cw
            moved = rolled(rolled(value, first - 1, 0), BLOCK * (spot - 1 - l), 1)
            out = jnp.where((block == spot) & (sub >= first) & (sub < first + plan.cw), moved, out)
    return out


def fold(value):
    half = value + pltpu.roll(value, 2 * BLOCK, 1)
    return half + pltpu.roll(half, BLOCK, 1)


def same(value, spot):
    return fold(jnp.where(iota(value.shape, 1) // BLOCK == spot, value, 0.0))


def dot(a, b, contract=((1,), (0,))):
    return lax.dot_general(a, b, (contract, ((), ())), precision=precise, preferred_element_type=F32)


def taken(value, index):
    return jnp.take_along_axis(value, index, axis=1, mode="promise_in_bounds")


def small_inverses(value):
    lane, sub = iota(value.shape, 1), iota(value.shape, 0)
    start = lane // REG * REG
    cols = [taken(value, start + j) for j in range(REG)]
    for k in range(REG):
        col = cols[k]
        here = sub == k
        recip = 1.0 / col[k : k + 1]
        left = jnp.where(here, -1.0, col)
        for j in range(REG):
            if j != k:
                row = cols[j][k : k + 1] * recip
                cols[j] = jnp.where(here, 0.0, cols[j]) - left * row
        cols[k] = jnp.where(here, recip, -col * recip)
    out = cols[0]
    for j in range(1, REG):
        out = jnp.where(lane % REG == j, cols[j], out)
    return out


def block_inverses(matrix, first, count):
    width = matrix.shape[1]
    lane, sub = iota((REG, width), 1), iota((REG, width), 0)
    value = jnp.where(lane % REG == sub, 1.0, 0.0)
    for q in range(first, first + count):
        value = jnp.where(lane // REG == q, matrix[q * REG : (q + 1) * REG], value)
    value = small_inverses(value)
    return jnp.concatenate([jnp.where(lane // REG == q, value, 0.0) for q in range(first, first + count)], axis=0)


def placed(value, first, total):
    pieces = []
    if first:
        pieces.append(jnp.zeros((first, value.shape[1]), F32))
    pieces.append(value)
    rest = total - first - value.shape[0]
    if rest:
        pieces.append(jnp.zeros((rest, value.shape[1]), F32))
    return jnp.concatenate(pieces, axis=0) if len(pieces) > 1 else value


def tail_inverse(matrix, first, count):
    size = matrix.shape[0]
    if count == 1:
        return block_inverses(matrix, first, 1)
    a, b, c = first * REG, (first + count // 2) * REG, (first + count) * REG
    lane = iota((1, size), 1)
    early, late = (lane >= a) & (lane < b), (lane >= b) & (lane < c)
    x = block_inverses(matrix, first, count // 2)
    f = placed(jnp.where(late, matrix[a:b], 0.0), a, size)
    y = dot(x, f)
    y_full = placed(y, a, size)
    rest = matrix[b:c] - dot(jnp.where(early, matrix[b:c], 0.0), y_full)
    rest = jnp.where(late, rest, 0.0)
    inner = tail_inverse(placed(rest, b, size), first + count // 2, count // 2)
    t = dot(y, placed(inner, b, size))
    top = jnp.where(early, x + dot(t, y_full, ((1,), (1,))), -t)
    turned = placed(t, a, size).T
    low = jnp.where(early, -turned[b:c], inner)
    return jnp.concatenate([top, low], axis=0)


def whole_inverse(matrix, between):
    half = matrix.shape[0] // 2
    x = block_inverses(matrix[:half, :half], 0, half // REG)
    y = dot(x, matrix[:half, half:])
    rest = matrix[half:, half:] - dot(matrix[half:, :half], y)
    inner = tail_inverse(rest, 0, half // REG)
    between()
    t = dot(y, inner)
    top = jnp.concatenate([x + dot(t, y, ((1,), (1,))), -t], axis=1)
    return jnp.concatenate([top, jnp.concatenate([-t.T, inner], axis=1)], axis=0)


def region_of(at):
    q = at // REG
    row = jnp.where(q < 8, 2 * q, jnp.where(q < 12, 4 * q - 31, jnp.where(q < 14, 8 * q - 93, jnp.where(q < 15, 7, 15))))
    return row * REG + at % REG


def coarse_matrix(value, first):
    size = value.shape[0]
    gap = region_of(iota((size, size), 1)) - region_of(iota((size, size), 0))
    total = jnp.zeros((size, size), F32)
    for k in range(9):
        total = jnp.where(gap == REG * (k // 3 - 1) + k % 3 - 1, value[:, first + k : first + k + 1], total)
    return total


def banded(diag_ref, pad_ref):
    out = []
    for q in range(REG):
        total = None
        for k in range(9):
            row = ORDER[q] + k // 3 - 1
            if 0 <= row < REG:
                at = 8 + REG * ORDER.index(row) + k % 3 - 1
                term = diag_ref[k, q * REG : (q + 1) * REG, :] * pad_ref[at : at + REG, :]
                total = term if total is None else total + term
        out.append(total)
    return jnp.concatenate(out, axis=0)


def wide(value):
    return jnp.broadcast_to(value, (LANES, LANES)).T[:BLOCK]


def front_kernel(
    plan, b_hbm, h_ref, v_ref, label_ref, bump_ref, pad_class_ref, edge_table, pad_table,
    b1_out, b2_out, planes_out, cx_ref, wide_ref,
    braw, bt, u0, u1, b1, b2, planes, ea, eb, ec, ga, gb, gc, brow, bcol, ccol, cpack, cpack1, hp,
    s0, s1, s2, s3, s4, pa, pb, pc, tacc,
    set0, set1, set2, side0, side1, side2, gset0, gset1, gset2, gside0, gside1, gside2,
    note, gat, q0, q1, q2, cpad, diag, knat,
    in_sem, out_sem, send_sem, recv_sem, note_send, note_recv,
):
    rows, cols, n, hn = plan.rows, plan.cols, plan.loads, plan.half
    r, c = lax.axis_index("row"), lax.axis_index("col")
    me = r * plan.nc + c
    count = plan.count
    barrier = pltpu.get_barrier_semaphore()

    def device(d):
        other = lax.rem(me + d, count)
        return (other // plan.nc, lax.rem(other, plan.nc))

    def fetch(k):
        return pltpu.make_async_copy(b_hbm.at[k], braw.at[pl.ds(pl.multiple_of(k * plan.pitch, 8), rows)], in_sem.at[k])

    def fetch_start(k, carry):
        fetch(k).start()
        return carry

    def fetch_wait(k, carry):
        fetch(k).wait()
        return carry

    lax.fori_loop(0, n, fetch_start, 0)
    for ref in (ga, gb, gc, brow, bcol, ccol, gset0, gset1, gset2, gside0, gside1, gside2):
        ref[...] = jnp.zeros_like(ref)
    u1[0:n, :] = jnp.zeros((n, cols), F32)
    u1[(rows + 1) * n :, :] = jnp.zeros((n, cols), F32)

    def greet(d, carry):
        pl.semaphore_signal(barrier, inc=1, device_id=device(d), device_id_type=pl.DeviceIdType.MESH)
        return carry

    lax.fori_loop(1, count, greet, 0)

    i, j = iota((rows, cols), 0), iota((rows, cols), 1)
    row_end = jnp.where(r == plan.nr - 1, rows - 1, rows)
    col_end = jnp.where(c == plan.nc - 1, cols - 1, cols)
    planes[CO + 1] = jnp.where(j == col_end, 0.0, looked_up(edge_table, h_ref[...]))
    planes[CO + 3] = jnp.where(i == row_end, 0.0, looked_up(edge_table, v_ref[...]))
    for ref in (ea, eb, ec):
        ref[...] = jnp.zeros_like(ref)
    put_edges(ea, 0, label_ref[...].astype(F32))
    put_edges(ea, 1, bump_ref[...])
    put_edges(ea, 2, planes[CO + 1])
    put_edges(ea, 3, planes[CO + 3])
    legs = Legs(plan, send_sem, recv_sem)
    first_edges = legs.make(beside(ea, ga))
    base_row, base_col = windows(plan)
    bump = bump_ref[...]
    for k, hit in enumerate(hits_of(label_ref[...].astype(F32), base_row, base_col)):
        planes[Z + k] = jnp.where(hit, bump, 0.0)
    pl.semaphore_wait(barrier, count - 1)
    legs.start(first_edges)

    for ref in (s0, s1, s2, s3, s4, pa, pb, pc):
        ref[...] = jnp.zeros_like(ref)
    lax.fori_loop(0, n, fetch_wait, 0)

    def packs(pack, value, k):
        left, right = pack
        lane = iota(value.shape, 1)
        moved = pltpu.roll(value, k, 1)
        return jnp.where(lane == k, moved, left), jnp.where(lane == lax.rem(k + cols - 1, cols), moved, right)

    zero = jnp.zeros((hn, cols), F32)
    for h in (0, 1):
        pack = (zero, zero)
        for part, first, last in plan.chunks():

            def step(k, u, carry):
                acc, pack = carry
                v = braw[pl.ds(k + h * hn * plan.pitch, hn, stride=plan.pitch), :]
                bt[pl.ds(pl.multiple_of(k * n + h * hn, 8), hn), :] = v
                return tuple(x + row_of(planes, Z + m, k) * v for m, x in enumerate(acc)), packs(pack, v, k)

            acc, pack = over_rows(first, last, step, ((zero,) * 4, pack))
            add_sums(plan, s0, h, part, acc)
        cpack[0, h * hn : (h + 1) * hn, :] = pack[1]
        cpack[1, h * hn : (h + 1) * hn, :] = pack[0]
    load_edges = legs.make([
        (1, 0, bt.at[pl.ds((rows - 1) * n, n)], brow.at[0]),
        (-1, 0, bt.at[pl.ds(0, n)], brow.at[1]),
        (0, 1, cpack.at[0], bcol.at[0]),
        (0, -1, cpack.at[1], bcol.at[1]),
    ])
    legs.start(load_edges)

    legs.wait(first_edges)
    around = Around(ga, rows, cols)
    right, down = planes[CO + 1], planes[CO + 3]
    left, upper = around.left(right, 2), around.top(down, 3)
    diagonal = looked_up(pad_table, pad_class_ref[...]) + right + left + down + upper
    minv = 1.0 / diagonal
    planes[CO] = diagonal
    planes[CO + 2] = left
    planes[CO + 4] = upper
    planes[MINV] = minv
    named = label_ref[...].astype(F32)
    bump = bump_ref[...]
    total = None
    for label, weight in (
        (named, diagonal * bump),
        (around.right(named, 0), -right * around.right(bump, 1)),
        (around.left(named, 0), -left * around.left(bump, 1)),
        (around.low(named, 0), -down * around.low(bump, 1)),
        (around.top(named, 0), -upper * around.top(bump, 1)),
    ):
        terms = [jnp.where(hit, weight, 0.0) for hit in hits_of(label, base_row, base_col)]
        total = terms if total is None else [t + u for t, u in zip(total, terms)]
    put_edges(eb, 0, minv)
    for k in range(4):
        planes[W0 + k] = total[k]
        value = total[k] * minv
        planes[V0 + k] = value
        put_edges(eb, 1 + k, value)
    image_edges = legs.make(beside(eb, gb))
    legs.start(image_edges)

    pair_sums(plan, planes, Z, W0, pa, 0)
    spread0 = Spread(plan, legs, set0, side0, gset0, gside0)
    spread0.send([packed(plan, s0), packed(plan, pa)])

    for h in (0, 1):
        dots = zero
        for part, first, last in plan.chunks():

            def step(k, u, carry):
                dots, acc = carry
                v = bt[pl.ds(pl.multiple_of(k * n + h * hn, 8), hn), :]
                w = row_of(planes, MINV, k) * v
                u0[pl.ds(pl.multiple_of((k + 1) * n + h * hn, 8), hn), :] = w
                return dots + v * w, tuple(x + row_of(planes, V0 + m, k) * v for m, x in enumerate(acc))

            dots, acc = over_rows(first, last, step, (dots, (zero,) * 4))
            add_sums(plan, s1, h, part, acc)
        tacc[h * hn : (h + 1) * hn, :] = dots

    def note_copy(m, d):
        return pltpu.make_async_remote_copy(
            src_ref=note.at[m],
            dst_ref=gat.at[m, me],
            send_sem=note_send.at[m, d],
            recv_sem=note_recv.at[m, d],
            device_id=device(d),
            device_id_type=pl.DeviceIdType.MESH,
        )

    def tell(m, value):
        note[m] = value
        gat[m, pl.ds(me, 1)] = value[None]

        def go(d, carry):
            note_copy(m, d).start()
            return carry

        lax.fori_loop(1, count, go, 0)

    def hear(m):
        def go(d, carry):
            note_copy(m, d).wait()
            return carry

        lax.fori_loop(1, count, go, 0)

    load_sums, energy = spread0.merged()
    tell(0, message(plan, [(0, load_sums), (1, energy)]))

    def halo_columns(from_left, from_right):
        even = iota((n, cols), 1) % 2 == 0
        from_right = pltpu.roll(from_right, cols - 1, 1)
        hp[0] = jnp.where(even, from_left, from_right)
        hp[1] = jnp.where(even, from_right, from_left)

    legs.wait(load_edges)
    legs.wait(image_edges)
    u0[0:n, :] = brow[0] * gb[0, 0:1, :]
    u0[(rows + 1) * n :, :] = brow[1] * gb[1, 0:1, :]
    halo_columns(pltpu.roll(bcol[0], 1, 1) * gb[2, 0:1, :], bcol[1] * gb[3, 0:1, :])
    around = Around(gb, rows, cols)
    for k, value in enumerate(around.images(plan, planes, V0, 1)):
        planes[W1 + k] = value
        value = value * planes[MINV]
        planes[V1 + k] = value
        put_edges(ec, k, value)
    next_edges = legs.make(beside(ec, gc))
    legs.start(next_edges)

    lane = iota((hn, cols), 1)

    def stencil(field, h, k, u):
        def at(t):
            return field[pl.ds(pl.multiple_of(t * n + h * hn, 8), hn), :]

        z = at(k + 1)
        halo = pltpu.roll(hp[u % 2, h * hn : (h + 1) * hn, :], lax.rem(cols - k, cols), 1)
        before = jnp.where(lane == 0, halo, pltpu.roll(z, 1, 1))
        after = jnp.where(lane == cols - 1, halo, pltpu.roll(z, cols - 1, 1))
        f = (
            row_of(planes, CO, k) * z
            - row_of(planes, CO + 1, k) * after
            - row_of(planes, CO + 2, k) * before
            - row_of(planes, CO + 3, k) * at(k + 2)
            - row_of(planes, CO + 4, k) * at(k)
        )
        return z, f

    for h in (0, 1):
        pack, dots, more = (zero, zero), zero, zero
        for part, first, last in plan.chunks():

            def step(k, u, carry):
                dots, more, acc, bcc, pack = carry
                z, f = stencil(u0, h, k, u)
                w = row_of(planes, MINV, k) * f
                b1[pl.ds(pl.multiple_of(k * n + h * hn, 8), hn), :] = f
                u1[pl.ds(pl.multiple_of((k + 1) * n + h * hn, 8), hn), :] = w
                acc = tuple(x + row_of(planes, V0 + m, k) * f for m, x in enumerate(acc))
                bcc = tuple(x + row_of(planes, V1 + m, k) * f for m, x in enumerate(bcc))
                return dots + z * f, more + w * f, acc, bcc, packs(pack, w, k)

            dots, more, acc, bcc, pack = over_rows(first, last, step, (dots, more, (zero,) * 4, (zero,) * 4, pack))
            add_sums(plan, s2, h, part, acc)
            add_sums(plan, s3, h, part, bcc)
        tacc[n + h * hn : n + (h + 1) * hn, :] = dots
        tacc[2 * n + h * hn : 2 * n + (h + 1) * hn, :] = more
        cpack1[0, h * hn : (h + 1) * hn, :] = pack[1]
        cpack1[1, h * hn : (h + 1) * hn, :] = pack[0]
    field_edges = legs.make([
        (1, 0, u1.at[pl.ds(rows * n, n)], u1.at[pl.ds(0, n)]),
        (-1, 0, u1.at[pl.ds(n, n)], u1.at[pl.ds((rows + 1) * n, n)]),
        (0, 1, cpack1.at[0], ccol.at[0]),
        (0, -1, cpack1.at[1], ccol.at[1]),
    ])
    legs.start(field_edges)
    out1 = pltpu.make_async_copy(b1, b1_out, out_sem.at[0])
    out1.start()

    pair_sums(plan, planes, W0, V0, pb, 0)
    pair_sums(plan, planes, W1, V0, pb, 9)
    pair_sums(plan, planes, W1, V1, pb, 18)
    spread1 = Spread(plan, legs, set1, side1, gset1, gside1)
    spread1.send([packed(plan, s1), packed(plan, s2), packed(plan, s3), packed(plan, pb)])

    legs.wait(next_edges)
    around = Around(gc, rows, cols)
    for k, value in enumerate(around.images(plan, planes, V1, 0)):
        planes[W2 + k] = value
    out0 = pltpu.make_async_copy(planes.at[pl.ds(0, KEPT)], planes_out, out_sem.at[1])
    out0.start()
    legs.wait(field_edges)
    halo_columns(pltpu.roll(ccol[0], 1, 1), ccol[1])

    for h in (0, 1):
        dots = zero
        for part, first, last in plan.chunks():

            def step(k, u, carry):
                dots, acc = carry
                z, f = stencil(u1, h, k, u)
                b2[pl.ds(pl.multiple_of(k * n + h * hn, 8), hn), :] = f
                return dots + z * f, tuple(x + row_of(planes, V1 + m, k) * f for m, x in enumerate(acc))

            dots, acc = over_rows(first, last, step, (dots, (zero,) * 4))
            add_sums(plan, s4, h, part, acc)
        tacc[3 * n + h * hn : 3 * n + (h + 1) * hn, :] = dots
    out2 = pltpu.make_async_copy(b2, b2_out, out_sem.at[2])
    out2.start()
    pair_sums(plan, planes, W2, V1, pc, 0)
    spread2 = Spread(plan, legs, set2, side2, gset2, gside2)
    spread2.send([packed(plan, pc), packed(plan, s4)])
    dots = jnp.sum(tacc[...].T, axis=0, keepdims=True)

    first_sums, second_sums, third_sums, pairs = spread1.merged()
    tell(1, message(plan, [(0, first_sums), (1, second_sums), (2, third_sums), (3, pairs)]))

    def settle(m, ref):
        hear(m)
        for d in range(count):
            for l in range(plan.lv):
                at = REG * ORDER.index(d // plan.nc * plan.lv + l) + d % plan.nc * plan.cw
                ref[at : at + plan.cw, :] = gat[m, d, l * plan.cw : (l + 1) * plan.cw, :]

    def last_message():
        last_pairs, last_sums = spread2.merged()
        value = message(plan, [(0, last_pairs), (3, last_sums)])
        sub, block = iota((8, LANES), 0), iota((8, LANES), 1) // BLOCK
        for k in range(4):
            value = jnp.where((sub == k) & (block == 1), rolled(dots, BLOCK * (1 - k), 1), value)
        tell(2, value)

    settle(0, q0)
    inverse = whole_inverse(coarse_matrix(q0[...], BLOCK), last_message)
    c0 = same(dot(inverse, q0[...]), 0)
    settle(1, q1)
    settle(2, q2)

    regions = c0.shape[0]
    block = iota((regions, LANES), 1) // BLOCK
    pair_values = jnp.where(block == 3, q1[...], q2[...])
    sums = jnp.where(block == 3, q2[...], q1[...])
    start = jnp.where(block == 3, 0, 3 * BLOCK + 9 * block)
    for k in range(9):
        diag[k] = taken(pair_values, start + k)
    all_dots = jnp.sum(gat[2], axis=0)
    row_block = iota((1, LANES), 1) // BLOCK
    dots = jnp.zeros((1, LANES), F32)
    for k in range(4):
        dots = jnp.where(row_block == k, rolled(all_dots[k : k + 1], BLOCK * (k - 1), 1), dots)

    def over(value):
        return jnp.sum(value, axis=0, keepdims=True)

    cpad[...] = jnp.zeros_like(cpad)
    cpad[8 : 8 + regions, :] = c0
    reduced = sums - banded(diag, cpad)
    dots = dots - over(c0 * (sums + reduced))
    rho, m1, m2, m3 = [same(dots, k) for k in range(4)]
    solved = dot(inverse, reduced)
    c1, e2 = same(solved, 0), same(solved, 1)
    cpad[8 : 8 + regions, :] = c1
    image = banded(diag, cpad)
    in_c1 = over(c1 * reduced)
    image_c1 = over(c1 * image)
    with_s1, with_s2, with_s3 = [same(in_c1, k) for k in range(3)]
    curve = m1 - with_s1
    alpha = rho / curve
    square = m2 - 2.0 * with_s2 + same(image_c1, 0)
    turned = same(dot(inverse, image), 0)
    c2 = c1 - alpha * (e2 - turned)
    now = reduced - alpha * (pltpu.roll(reduced, 3 * BLOCK, 1) - image)
    in_c2 = same(over(c2 * now), 0)
    image_dot = m1 - 2.0 * alpha * (m2 - with_s2) + alpha * alpha * (m3 - 2.0 * with_s3 + same(image_c1, 1))
    rho1 = rho - 2.0 * alpha * curve + alpha * alpha * square
    beta = rho1 / rho
    curve1 = image_dot - in_c2 + 2.0 * beta * (curve - alpha * square) + beta * beta * curve
    alpha1 = rho1 / curve1
    mix = alpha + alpha1 * beta
    kappa, lam = mix + alpha1, alpha * alpha1
    coefs = jnp.where(block == 0, c0 - mix * c1 - alpha1 * c2, jnp.where(block == 1, lam * c1 - kappa * c0, lam * c0))
    wide_ref[0] = wide(kappa)
    wide_ref[1] = wide(lam)

    knat[...] = jnp.zeros_like(knat)
    for q in range(REG):
        at = REG * (1 + ORDER[q])
        knat[at : at + REG, :] = coefs[q * REG : (q + 1) * REG]
    near = knat[pl.ds(pl.multiple_of(r * (plan.lv * REG), REG), LANES), :].T
    base = c * plan.cw - 1 + (iota((3 * BLOCK, cols), 1) + plan.width // 2) // plan.width
    for b in (0, 1):
        column = jnp.clip(base + b, 0, REG - 1)
        for l in range(plan.levels):
            value = taken(near[: 3 * BLOCK], column + l * REG)
            for f in range(3):
                cx_ref[f, b, l * n : (l + 1) * n, :] = value[f * BLOCK : f * BLOCK + n]

    out0.wait()
    out1.wait()
    out2.wait()
    legs.finish()


def last_kernel(
    plan, b_hbm, b1_hbm, b2_hbm, planes_hbm, cx_ref, wide_ref, x_hbm, r_hbm,
    braw, b1, b2, planes, xs, rs, in_sem, out_sem,
):
    n, hn = plan.loads, plan.half
    flat_b = braw.reshape(n * plan.pitch, plan.cols)
    flat_x = xs.reshape(n * plan.pitch, plan.cols)
    flat_r = rs.reshape(n * plan.pitch, plan.cols)
    arrivals, departures = [], []
    for part, first, last in plan.chunks():
        here, flat = pl.ds(first, last - first), pl.ds(first * n, (last - first) * n)
        arrivals.append([
            pltpu.make_async_copy(src, dst, in_sem.at[part, k])
            for k, (src, dst) in enumerate((
                (planes_hbm.at[:, here], planes.at[:, here]),
                (b_hbm.at[:, here], braw.at[:, here]),
                (b1_hbm.at[flat], b1.at[flat]),
                (b2_hbm.at[flat], b2.at[flat]),
            ))
        ])
        departures.append([
            pltpu.make_async_copy(xs.at[:, here], x_hbm.at[:, here], out_sem.at[part, 0]),
            pltpu.make_async_copy(rs.at[:, here], r_hbm.at[:, here], out_sem.at[part, 1]),
        ])
    for copies in arrivals:
        for copy in copies:
            copy.start()
    for part, first, last in plan.chunks():
        for copy in arrivals[part]:
            copy.wait()
        for h in (0, 1):
            kappa, lam = [wide_ref[k, h * hn : (h + 1) * hn, :] for k in (0, 1)]
            cx = []
            for f in range(3):
                for a in (0, 1):
                    for b in (0, 1):
                        at = (part + a) * n + h * hn
                        cx.append(cx_ref[f, b, at : at + hn, :])

            def step(k, u, carry):
                at = pl.ds(pl.multiple_of(k * n + h * hn, 8), hn)
                to = pl.ds(k + h * hn * plan.pitch, hn, stride=plan.pitch)
                v0, v1, v2 = flat_b[to, :], b1[at, :], b2[at, :]
                x = kappa * v0 - lam * v1
                r = v0 - kappa * v1 + lam * v2
                plain = None
                for m in range(4):
                    w0 = row_of(planes, W0 + m, k)
                    w1 = row_of(planes, W1 + m, k)
                    x = x + w0 * cx[4 + m] + w1 * cx[8 + m]
                    r = r - w0 * cx[m] - w1 * cx[4 + m] - row_of(planes, W2 + m, k) * cx[8 + m]
                    term = row_of(planes, Z + m, k) * cx[m]
                    plain = term if plain is None else plain + term
                flat_x[to, :] = row_of(planes, MINV, k) * x + plain
                flat_r[to, :] = r
                return carry

            over_rows(first, last, step, 0, 4)
        for copy in departures[part]:
            copy.start()
    for copies in departures:
        for copy in copies:
            copy.wait()


def body(load_currents, labels, bump_height, horizontal_class, vertical_class, pad_class, edge_table, pad_table):
    rows, cols = labels.shape
    loads = load_currents.shape[0]
    nr, nc = lax.axis_size("row"), lax.axis_size("col")
    height, width = nr * rows // REG, nc * cols // REG
    plan = Plan(rows, cols, loads, height, width, nr, nc)
    n, regions, count = loads, REG * REG, plan.count
    field = (rows * n, cols)
    tall = ((rows + 2) * n, cols)
    edge = (4, 8, cols)
    sums = (2, LANES, cols)

    def vm(*dims):
        return pltpu.VMEM(dims, F32)

    def dma(*dims):
        return pltpu.SemaphoreType.DMA(dims)

    legs = 4 * 5 + 3 * 8
    b1, b2, planes, cx, scales = pl.pallas_call(
        functools.partial(front_kernel, plan),
        out_shape=(shape(*field), shape(*field), shape(KEPT, rows, cols), shape(3, 2, plan.levels * n, cols), shape(2, n, cols)),
        in_specs=[ANY] + [VM] * 5 + [SM] * 2,
        out_specs=(ANY, ANY, ANY, VM, VM),
        scratch_shapes=[
            vm(n * plan.pitch, cols), vm(*field), vm(*tall), vm(*tall), vm(*field), vm(*field), vm(PLANES, rows, cols),
            vm(*edge), vm(*edge), vm(*edge), vm(*edge), vm(*edge), vm(*edge),
            vm(2, n, cols), vm(2, n, cols), vm(2, n, cols), vm(2, n, cols), vm(2, n, cols), vm(2, n, cols),
        ] + [vm(*sums)] * 8 + [
            vm(LANES, LANES),
            vm(2, 8, LANES), vm(4, 8, LANES), vm(2, 8, LANES), vm(2, 8, LANES), vm(2, 8, LANES), vm(2, 8, LANES),
            vm(2, 2, 8, LANES), vm(2, 4, 8, LANES), vm(2, 2, 8, LANES), vm(6, 8, LANES), vm(6, 8, LANES), vm(6, 8, LANES),
            vm(3, 8, LANES), vm(3, count, 8, LANES), vm(regions, LANES), vm(regions, LANES), vm(regions, LANES),
            vm(regions + 16, LANES), vm(9, regions, LANES), vm(regions + LANES + 2 * REG, LANES),
            dma(n), dma(3), dma(legs), dma(legs), dma(3, count), dma(3, count),
        ],
        compiler_params=pltpu.CompilerParams(collective_id=0, has_side_effects=True, vmem_limit_bytes=56 * 1024 * 1024),
    )(load_currents, horizontal_class, vertical_class, labels, bump_height, pad_class, edge_table, pad_table)
    staged = (n, plan.pitch, cols)
    return pl.pallas_call(
        functools.partial(last_kernel, plan),
        out_shape=(shape(n, rows, cols),) * 2,
        in_specs=[ANY] * 4 + [VM] * 2,
        out_specs=(ANY, ANY),
        scratch_shapes=[
            vm(*staged), vm(*field), vm(*field), vm(KEPT, rows, cols), vm(*staged), vm(*staged),
            dma(plan.parts, 4), dma(plan.parts, 2),
        ],
        compiler_params=pltpu.CompilerParams(vmem_limit_bytes=56 * 1024 * 1024),
    )(load_currents, b1, b2, planes, cx, scales)


def solution(mesh):
    grid = P("row", "col")
    cube = P(None, "row", "col")
    return jax.shard_map(
        body,
        mesh=mesh,
        in_specs=(cube, grid, grid, grid, grid, grid, P(), P()),
        out_specs=(cube, cube),
        check_vma=False,
    )
```

time: 162 us -> 66.7 us (0.41)
  Pallas kernels: 156 us -> 65.9 us
  other arithmetic: 3.12 us -> 0 us
  local copies, waits for them, and re-layouts: 1.69 us -> 0 us
    pallas_call x18 -> x2, Pallas kernels: 156 us -> 65.9 us  [the longest x1 57 us: body(): pl.pallas_call(functools.partial(front_kernel, plan), out_shape=(shape(*f...]
    convert_element_type x2 -> x0, other arithmetic: 2.44 us -> none  [the longest x1 1.27 us: body(): ((here // REG == at_row) & (here % REG == at_col) & (x < span) & (level <...]
    another operation x1 -> x0, local copies, waits for them, and re-layouts: 1.69 us -> none  [body(): first[:, 1].reshape(count * 8, 4 * BLOCK)]
where the time goes in v1:
time: 66.7 us; the launch traced here: 66.5 us
  Pallas kernels  65.9 us (99%)
    pallas_call x1, Pallas kernels, body(): pl.pallas_call(functools.partial(front_kernel, plan), out_shape=(shape(*f...  57 us
    pallas_call x1, Pallas kernels, body(): pl.pallas_call(functools.partial(last_kernel, plan), out_shape=(shape(n,...  8.83 us

profile of v1, /device:TPU:0, one launch (start us, length us, event | category | flops | bytes accessed | tf_op | source)
XLA Modules:
  0.0 66.5 jit_solution(1570614529587140448)
XLA Ops:
  0.6 57.0 %shard_map.95 = (f32[4096,128]{1,0:T(8,128)}, f32[4096,128]{1,0:T(8,128)}, f32[17,128,128]{2,1,0:T(8,128)}, f32[3,2,128,128]{3,2,1,0:T(8,128)}, f32[2,32,128]{2,1,0:T(8,128)}) custom-call(f32[32,128,128]{2,1,0:T(8,128)} %b_hbm.3, s32[128,128]{1,0:T(8,128)} %h_ref.1, s32[128,128]{1,0:T(8,128)} %v_ref.1, s32[128,128]{1,0:T(8,128)} %label_ref.1, ...), custom_call_target="tpu_custom_call" | custom-call | tf_op jit(solution)/shard_map/pallas_call | solution.py:872
  57.7 8.8 %shard_map.96 = (f32[32,128,128]{2,1,0:T(8,128)}, f32[32,128,128]{2,1,0:T(8,128)}) custom-call(f32[32,128,128]{2,1,0:T(8,128)} %b_hbm.3, f32[4096,128]{1,0:T(8,128)} %get-tuple-element.7.b1_hbm, f32[4096,128]{1,0:T(8,128)} %get-tuple-element.8.b2_hbm, f32[17,128,128]{2,1,0:T(8,128)} %get-tuple-element.9.planes_hbm, ...), custom_call_target="tpu_custom_call" | custom-call | tf_op jit(solution)/shard_map/pallas_call | solution.py:892

commit v2 on v1

--- a/solution.py
+++ b/solution.py
@@ -16,8 +16,10 @@
 BLOCK = 32
 LANES = 4 * BLOCK
 PITCH = 8
+GROUP = 32
 MINV, Z, W0, W1, W2, V0, V1, CO = 0, 1, 5, 9, 13, 17, 21, 25
-KEPT, PLANES = 17, 30
+KEPT, PLANES = 17, 32
+RIGHT_IN, LEFT_IN = 30, 31
 ORDER = (0, 2, 4, 6, 8, 10, 12, 14, 1, 5, 9, 13, 3, 11, 7, 15)
 
 
@@ -59,6 +61,10 @@
         return carry
 
     return lax.fori_loop(0, (last - first) // group, body, init)
+
+
+def over_groups(first, last, group, init, size=8):
+    return lax.fori_loop(0, (last - first) // size, lambda g, carry: group(first + g * size, carry), init)
 
 
 def row_of(ref, k, i):
@@ -376,8 +382,8 @@
     x = block_inverses(matrix[:half, :half], 0, half // REG)
     y = dot(x, matrix[:half, half:])
     rest = matrix[half:, half:] - dot(matrix[half:, :half], y)
+    between()
     inner = tail_inverse(rest, 0, half // REG)
-    between()
     t = dot(y, inner)
     top = jnp.concatenate([x + dot(t, y, ((1,), (1,))), -t], axis=1)
     return jnp.concatenate([top, jnp.concatenate([-t.T, inner], axis=1)], axis=0)
@@ -419,7 +425,7 @@
 def front_kernel(
     plan, b_hbm, h_ref, v_ref, label_ref, bump_ref, pad_class_ref, edge_table, pad_table,
     b1_out, b2_out, planes_out, cx_ref, wide_ref,
-    braw, bt, u0, u1, b1, b2, planes, ea, eb, ec, ga, gb, gc, brow, bcol, ccol, cpack, cpack1, hp,
+    braw, bt, u0, u1, b1, b2, planes, ea, eb, ec, ga, gb, gc, brow, bcol, ccol, cpack, cpack1, beyond,
     s0, s1, s2, s3, s4, pa, pb, pc, tacc,
     set0, set1, set2, side0, side1, side2, gset0, gset1, gset2, gside0, gside1, gside2,
     note, gat, q0, q1, q2, cpad, diag, knat,
@@ -482,27 +488,47 @@
         ref[...] = jnp.zeros_like(ref)
     lax.fori_loop(0, n, fetch_wait, 0)
 
-    def packs(pack, value, k):
-        left, right = pack
-        lane = iota(value.shape, 1)
-        moved = pltpu.roll(value, k, 1)
-        return jnp.where(lane == k, moved, left), jnp.where(lane == lax.rem(k + cols - 1, cols), moved, right)
-
+    lane = iota((hn, cols), 1)
+    even = lane % 2 == 0
     zero = jnp.zeros((hn, cols), F32)
+
+    def own(h):
+        return slice(h * hn, (h + 1) * hn)
+
+    def spot(h, k):
+        return pl.ds(pl.multiple_of(k * n + h * hn, 8), hn)
+
+    def keep_ends(ref, h, field, skip):
+        pack, top = [zero, zero], None
+        for k in range(rows):
+            moved = rolled(field[spot(h, k + skip), :], k, 1)
+            top = moved if k == 0 else top
+            pack[k % 2] = moved if k < 2 else jnp.where(lane >= k - 1, moved, pack[k % 2])
+        pack[0] = jnp.where(lane == cols - 1, top, pack[0])
+        ref[0, own(h), :] = jnp.where(even, pack[1], pack[0])
+        ref[1, own(h), :] = jnp.where(even, pack[0], pack[1])
+
+    def halo_rows(h, from_left, from_right):
+        from_left = -ga[2, 2:3, :] * from_left
+        from_right = pltpu.roll(-ea[2, 2:3, :] * from_right, cols - 1, 1)
+        pair = [jnp.where(even, from_left, from_right), jnp.where(even, from_right, from_left)]
+        outer = (lane == 0) | (lane == cols - 1)
+        for k in range(rows):
+            beyond[spot(h, k), :] = jnp.where(outer, rolled(pair[k % 2], -k, 1), 0.0)
+
     for h in (0, 1):
-        pack = (zero, zero)
         for part, first, last in plan.chunks():
 
-            def step(k, u, carry):
-                acc, pack = carry
-                v = braw[pl.ds(k + h * hn * plan.pitch, hn, stride=plan.pitch), :]
-                bt[pl.ds(pl.multiple_of(k * n + h * hn, 8), hn), :] = v
-                return tuple(x + row_of(planes, Z + m, k) * v for m, x in enumerate(acc)), packs(pack, v, k)
-
-            acc, pack = over_rows(first, last, step, ((zero,) * 4, pack))
-            add_sums(plan, s0, h, part, acc)
-        cpack[0, h * hn : (h + 1) * hn, :] = pack[1]
-        cpack[1, h * hn : (h + 1) * hn, :] = pack[0]
+            def group(base, acc):
+                for u in range(8):
+                    k = base + u
+                    v = braw[pl.ds(k + h * hn * plan.pitch, hn, stride=plan.pitch), :]
+                    bt[spot(h, k), :] = v
+                    acc = tuple(x + row_of(planes, Z + m, k) * v for m, x in enumerate(acc))
+                return acc
+
+            add_sums(plan, s0, h, part, over_groups(first, last, group, (zero,) * 4))
+        keep_ends(cpack, h, bt, 0)
     load_edges = legs.make([
         (1, 0, bt.at[pl.ds((rows - 1) * n, n)], brow.at[0]),
         (-1, 0, bt.at[pl.ds(0, n)], brow.at[1]),
@@ -519,6 +545,8 @@
     minv = 1.0 / diagonal
     planes[CO] = diagonal
     planes[CO + 2] = left
+    planes[RIGHT_IN] = jnp.where(j == cols - 1, 0.0, right)
+    planes[LEFT_IN] = jnp.where(j == 0, 0.0, left)
     planes[CO + 4] = upper
     planes[MINV] = minv
     named = label_ref[...].astype(F32)
@@ -552,9 +580,9 @@
 
             def step(k, u, carry):
                 dots, acc = carry
-                v = bt[pl.ds(pl.multiple_of(k * n + h * hn, 8), hn), :]
+                v = bt[spot(h, k), :]
                 w = row_of(planes, MINV, k) * v
-                u0[pl.ds(pl.multiple_of((k + 1) * n + h * hn, 8), hn), :] = w
+                u0[spot(h, k + 1), :] = w
                 return dots + v * w, tuple(x + row_of(planes, V0 + m, k) * v for m, x in enumerate(acc))
 
             dots, acc = over_rows(first, last, step, (dots, (zero,) * 4))
@@ -588,20 +616,12 @@
 
         lax.fori_loop(1, count, go, 0)
 
-    load_sums, energy = spread0.merged()
-    tell(0, message(plan, [(0, load_sums), (1, energy)]))
-
-    def halo_columns(from_left, from_right):
-        even = iota((n, cols), 1) % 2 == 0
-        from_right = pltpu.roll(from_right, cols - 1, 1)
-        hp[0] = jnp.where(even, from_left, from_right)
-        hp[1] = jnp.where(even, from_right, from_left)
-
     legs.wait(load_edges)
     legs.wait(image_edges)
     u0[0:n, :] = brow[0] * gb[0, 0:1, :]
     u0[(rows + 1) * n :, :] = brow[1] * gb[1, 0:1, :]
-    halo_columns(pltpu.roll(bcol[0], 1, 1) * gb[2, 0:1, :], bcol[1] * gb[3, 0:1, :])
+    for h in (0, 1):
+        halo_rows(h, pltpu.roll(bcol[0, own(h), :], 1, 1) * gb[2, 0:1, :], bcol[1, own(h), :] * gb[3, 0:1, :])
     around = Around(gb, rows, cols)
     for k, value in enumerate(around.images(plan, planes, V0, 1)):
         planes[W1 + k] = value
@@ -611,53 +631,52 @@
     next_edges = legs.make(beside(ec, gc))
     legs.start(next_edges)
 
-    lane = iota((hn, cols), 1)
-
-    def stencil(field, h, k, u):
-        def at(t):
-            return field[pl.ds(pl.multiple_of(t * n + h * hn, 8), hn), :]
-
-        z = at(k + 1)
-        halo = pltpu.roll(hp[u % 2, h * hn : (h + 1) * hn, :], lax.rem(cols - k, cols), 1)
-        before = jnp.where(lane == 0, halo, pltpu.roll(z, 1, 1))
-        after = jnp.where(lane == cols - 1, halo, pltpu.roll(z, cols - 1, 1))
+    def stencil(field, h, k):
+        z = field[spot(h, k + 1), :]
         f = (
             row_of(planes, CO, k) * z
-            - row_of(planes, CO + 1, k) * after
-            - row_of(planes, CO + 2, k) * before
-            - row_of(planes, CO + 3, k) * at(k + 2)
-            - row_of(planes, CO + 4, k) * at(k)
+            - row_of(planes, RIGHT_IN, k) * pltpu.roll(z, cols - 1, 1)
+            - row_of(planes, LEFT_IN, k) * pltpu.roll(z, 1, 1)
+            - row_of(planes, CO + 3, k) * field[spot(h, k + 2), :]
+            - row_of(planes, CO + 4, k) * field[spot(h, k), :]
         )
-        return z, f
-
+        return z, f + beyond[spot(h, k), :]
+
+    field_edges = []
     for h in (0, 1):
-        pack, dots, more = (zero, zero), zero, zero
+        dots, more = zero, zero
         for part, first, last in plan.chunks():
 
-            def step(k, u, carry):
-                dots, more, acc, bcc, pack = carry
-                z, f = stencil(u0, h, k, u)
-                w = row_of(planes, MINV, k) * f
-                b1[pl.ds(pl.multiple_of(k * n + h * hn, 8), hn), :] = f
-                u1[pl.ds(pl.multiple_of((k + 1) * n + h * hn, 8), hn), :] = w
-                acc = tuple(x + row_of(planes, V0 + m, k) * f for m, x in enumerate(acc))
-                bcc = tuple(x + row_of(planes, V1 + m, k) * f for m, x in enumerate(bcc))
-                return dots + z * f, more + w * f, acc, bcc, packs(pack, w, k)
-
-            dots, more, acc, bcc, pack = over_rows(first, last, step, (dots, more, (zero,) * 4, (zero,) * 4, pack))
+            def group(base, carry):
+                dots, more, acc, bcc = carry
+                for u in range(GROUP):
+                    k = base + u
+                    z, f = stencil(u0, h, k)
+                    w = row_of(planes, MINV, k) * f
+                    b1[spot(h, k), :] = f
+                    u1[spot(h, k + 1), :] = w
+                    acc = tuple(x + row_of(planes, V0 + m, k) * f for m, x in enumerate(acc))
+                    bcc = tuple(x + row_of(planes, V1 + m, k) * f for m, x in enumerate(bcc))
+                    dots, more = dots + z * f, more + w * f
+                return dots, more, acc, bcc
+
+            dots, more, acc, bcc = over_groups(first, last, group, (dots, more, (zero,) * 4, (zero,) * 4), GROUP)
             add_sums(plan, s2, h, part, acc)
             add_sums(plan, s3, h, part, bcc)
         tacc[n + h * hn : n + (h + 1) * hn, :] = dots
         tacc[2 * n + h * hn : 2 * n + (h + 1) * hn, :] = more
-        cpack1[0, h * hn : (h + 1) * hn, :] = pack[1]
-        cpack1[1, h * hn : (h + 1) * hn, :] = pack[0]
-    field_edges = legs.make([
-        (1, 0, u1.at[pl.ds(rows * n, n)], u1.at[pl.ds(0, n)]),
-        (-1, 0, u1.at[pl.ds(n, n)], u1.at[pl.ds((rows + 1) * n, n)]),
-        (0, 1, cpack1.at[0], ccol.at[0]),
-        (0, -1, cpack1.at[1], ccol.at[1]),
-    ])
-    legs.start(field_edges)
+        keep_ends(cpack1, h, u1, 1)
+        mine = pl.ds(h * hn, hn)
+        field_edges.append(legs.make([
+            (1, 0, u1.at[pl.ds(rows * n + h * hn, hn)], u1.at[pl.ds(h * hn, hn)]),
+            (-1, 0, u1.at[pl.ds(n + h * hn, hn)], u1.at[pl.ds((rows + 1) * n + h * hn, hn)]),
+            (0, 1, cpack1.at[0, mine], ccol.at[0, mine]),
+            (0, -1, cpack1.at[1, mine], ccol.at[1, mine]),
+        ]))
+        legs.start(field_edges[h])
+        if h == 0:
+            load_sums, energy = spread0.merged()
+            tell(0, message(plan, [(0, load_sums), (1, energy)]))
     out1 = pltpu.make_async_copy(b1, b1_out, out_sem.at[0])
     out1.start()
 
@@ -673,20 +692,23 @@
         planes[W2 + k] = value
     out0 = pltpu.make_async_copy(planes.at[pl.ds(0, KEPT)], planes_out, out_sem.at[1])
     out0.start()
-    legs.wait(field_edges)
-    halo_columns(pltpu.roll(ccol[0], 1, 1), ccol[1])
-
     for h in (0, 1):
+        legs.wait(field_edges[h])
+        halo_rows(h, pltpu.roll(ccol[0, own(h), :], 1, 1), ccol[1, own(h), :])
         dots = zero
         for part, first, last in plan.chunks():
 
-            def step(k, u, carry):
+            def group(base, carry):
                 dots, acc = carry
-                z, f = stencil(u1, h, k, u)
-                b2[pl.ds(pl.multiple_of(k * n + h * hn, 8), hn), :] = f
-                return dots + z * f, tuple(x + row_of(planes, V1 + m, k) * f for m, x in enumerate(acc))
-
-            dots, acc = over_rows(first, last, step, (dots, (zero,) * 4))
+                for u in range(GROUP):
+                    k = base + u
+                    z, f = stencil(u1, h, k)
+                    b2[spot(h, k), :] = f
+                    dots = dots + z * f
+                    acc = tuple(x + row_of(planes, V1 + m, k) * f for m, x in enumerate(acc))
+                return dots, acc
+
+            dots, acc = over_groups(first, last, group, (dots, (zero,) * 4), GROUP)
             add_sums(plan, s4, h, part, acc)
         tacc[3 * n + h * hn : 3 * n + (h + 1) * hn, :] = dots
     out2 = pltpu.make_async_copy(b2, b2_out, out_sem.at[2])
@@ -868,7 +890,7 @@
     def dma(*dims):
         return pltpu.SemaphoreType.DMA(dims)
 
-    legs = 4 * 5 + 3 * 8
+    legs = 4 * 6 + 3 * 8
     b1, b2, planes, cx, scales = pl.pallas_call(
         functools.partial(front_kernel, plan),
         out_shape=(shape(*field), shape(*field), shape(KEPT, rows, cols), shape(3, 2, plan.levels * n, cols), shape(2, n, cols)),
@@ -877,7 +899,7 @@
         scratch_shapes=[
             vm(n * plan.pitch, cols), vm(*field), vm(*tall), vm(*tall), vm(*field), vm(*field), vm(PLANES, rows, cols),
             vm(*edge), vm(*edge), vm(*edge), vm(*edge), vm(*edge), vm(*edge),
-            vm(2, n, cols), vm(2, n, cols), vm(2, n, cols), vm(2, n, cols), vm(2, n, cols), vm(2, n, cols),
+            vm(2, n, cols), vm(2, n, cols), vm(2, n, cols), vm(2, n, cols), vm(2, n, cols), vm(*field),
         ] + [vm(*sums)] * 8 + [
             vm(LANES, LANES),
             vm(2, 8, LANES), vm(4, 8, LANES), vm(2, 8, LANES), vm(2, 8, LANES), vm(2, 8, LANES), vm(2, 8, LANES),

time: 66.7 us -> 49.5 us (0.74)
  Pallas kernels: 65.9 us -> 48.5 us
    pallas_call x1, Pallas kernels: 57 us -> 39.7 us  [body(): pl.pallas_call(functools.partial(front_kernel, plan), out_shape=(shape(*f...]
where the time goes in v2:
time: 49.5 us; the launch traced here: 49.3 us
  Pallas kernels  48.5 us (98%)
  between operations  0.8 us (2%)
    pallas_call x1, Pallas kernels, body(): pl.pallas_call(functools.partial(front_kernel, plan), out_shape=(shape(*f...  39.7 us
    pallas_call x1, Pallas kernels, body(): pl.pallas_call(functools.partial(last_kernel, plan), out_shape=(shape(n,...  8.83 us

profile of v2, /device:TPU:0, one launch (start us, length us, event | category | flops | bytes accessed | tf_op | source)
XLA Modules:
  0.0 49.3 jit_solution(6124063141498088826)
XLA Ops:
  0.6 39.7 %shard_map.95 = (f32[4096,128]{1,0:T(8,128)}, f32[4096,128]{1,0:T(8,128)}, f32[17,128,128]{2,1,0:T(8,128)}, f32[3,2,128,128]{3,2,1,0:T(8,128)}, f32[2,32,128]{2,1,0:T(8,128)}) custom-call(f32[32,128,128]{2,1,0:T(8,128)} %b_hbm.3, s32[128,128]{1,0:T(8,128)} %h_ref.1, s32[128,128]{1,0:T(8,128)} %v_ref.1, s32[128,128]{1,0:T(8,128)} %label_ref.1, ...), custom_call_target="tpu_custom_call" | custom-call | tf_op jit(solution)/shard_map/pallas_call | solution.py:894
  40.3 8.8 %shard_map.96 = (f32[32,128,128]{2,1,0:T(8,128)}, f32[32,128,128]{2,1,0:T(8,128)}) custom-call(f32[32,128,128]{2,1,0:T(8,128)} %b_hbm.3, f32[4096,128]{1,0:T(8,128)} %get-tuple-element.7.b1_hbm, f32[4096,128]{1,0:T(8,128)} %get-tuple-element.8.b2_hbm, f32[17,128,128]{2,1,0:T(8,128)} %get-tuple-element.9.planes_hbm, ...), custom_call_target="tpu_custom_call" | custom-call | tf_op jit(solution)/shard_map/pallas_call | solution.py:914

commit v3 on v2

--- a/solution.py
+++ b/solution.py
@@ -9,10 +9,7 @@
 
 REG = 16
 F32 = jnp.float32
-precise = lax.Precision.HIGHEST
-VM = pl.BlockSpec(memory_space=pltpu.VMEM)
-SM = pl.BlockSpec(memory_space=pltpu.SMEM)
-ANY = pl.BlockSpec(memory_space=pl.ANY)
+HBM = pl.BlockSpec(memory_space=pltpu.HBM)
 BLOCK = 32
 LANES = 4 * BLOCK
 PITCH = 8
@@ -53,6 +50,13 @@
         for part in range(self.parts):
             yield part, max(0, part * self.height - half), min(self.rows, part * self.height + half)
 
+    def pieces(self):
+        for part, first, last in self.chunks():
+            cut = first + 8 if part == 0 else last - 8 if part == self.parts - 1 else first
+            for start, stop in ((first, cut), (cut, last)):
+                if stop > start:
+                    yield part, start, stop
+
 
 def over_rows(first, last, step, init, group=4):
     def body(g, carry):
@@ -76,27 +80,25 @@
         self.plan, self.send_sem, self.recv_sem = plan, send_sem, recv_sem
         self.used = 0
         self.r, self.c = lax.axis_index("row"), lax.axis_index("col")
-        self.everything = []
 
     def inside(self, dr, dc):
         r, c = self.r + dr, self.c + dc
         return (r >= 0) & (r < self.plan.nr) & (c >= 0) & (c < self.plan.nc)
 
-    def make(self, items):
+    def make(self, items, sends):
         out = []
         for dr, dc, src, dst in items:
             target = (lax.rem(self.r + dr + self.plan.nr, self.plan.nr), lax.rem(self.c + dc + self.plan.nc, self.plan.nc))
             copy = pltpu.make_async_remote_copy(
                 src_ref=src,
                 dst_ref=dst,
-                send_sem=self.send_sem.at[self.used],
+                send_sem=self.send_sem.at[sends + len(out)],
                 recv_sem=self.recv_sem.at[self.used],
                 device_id=target,
                 device_id_type=pl.DeviceIdType.MESH,
             )
             self.used += 1
             out.append((self.inside(dr, dc), self.inside(-dr, -dc), copy))
-        self.everything += out
         return out
 
     def start(self, legs):
@@ -107,8 +109,8 @@
         for _, comes, copy in legs:
             pl.when(comes)(copy.wait_recv)
 
-    def finish(self):
-        for goes, _, copy in self.everything:
+    def sent(self, legs):
+        for goes, _, copy in legs:
             pl.when(goes)(copy.wait_send)
 
 
@@ -257,7 +259,7 @@
             (0, 1, east, got_sides.at[3]),
             (1, 1, east, got_sides.at[4]),
             (-1, 1, east, got_sides.at[5]),
-        ])
+        ], 12)
 
     def send(self, values):
         last = self.plan.cw + 1
@@ -273,8 +275,10 @@
         shift = lv * BLOCK
         return own + jnp.where(block == 1, rolled(above, -shift, 1), 0.0) + jnp.where(block == lv, rolled(below, shift, 1), 0.0)
 
-    def merged(self):
+    def merged(self, early=False):
         self.legs.wait(self.mine)
+        if not early:
+            self.legs.sent(self.mine)
         sub = iota((8, LANES), 0)
         sides = self.got_sides
         right = self.meet(sides[0], sides[1], sides[2])
@@ -307,8 +311,18 @@
     return fold(jnp.where(iota(value.shape, 1) // BLOCK == spot, value, 0.0))
 
 
+def halves(value):
+    high = value.astype(jnp.bfloat16)
+    return high, (value - high.astype(F32)).astype(jnp.bfloat16)
+
+
 def dot(a, b, contract=((1,), (0,))):
-    return lax.dot_general(a, b, (contract, ((), ())), precision=precise, preferred_element_type=F32)
+    (a_high, a_low), (b_high, b_low) = halves(a), halves(b)
+    total = None
+    for left, right in ((a_high, b_low), (a_low, b_high), (a_high, b_high)):
+        term = lax.dot_general(left, right, (contract, ((), ())), preferred_element_type=F32)
+        total = term if total is None else total + term
+    return total
 
 
 def taken(value, index):
@@ -356,7 +370,7 @@
     return jnp.concatenate(pieces, axis=0) if len(pieces) > 1 else value
 
 
-def tail_inverse(matrix, first, count):
+def tail_inverse(matrix, first, count, between):
     size = matrix.shape[0]
     if count == 1:
         return block_inverses(matrix, first, 1)
@@ -369,7 +383,9 @@
     y_full = placed(y, a, size)
     rest = matrix[b:c] - dot(jnp.where(early, matrix[b:c], 0.0), y_full)
     rest = jnp.where(late, rest, 0.0)
-    inner = tail_inverse(placed(rest, b, size), first + count // 2, count // 2)
+    if count == 2:
+        between()
+    inner = tail_inverse(placed(rest, b, size), first + count // 2, count // 2, between)
     t = dot(y, placed(inner, b, size))
     top = jnp.where(early, x + dot(t, y_full, ((1,), (1,))), -t)
     turned = placed(t, a, size).T
@@ -382,8 +398,7 @@
     x = block_inverses(matrix[:half, :half], 0, half // REG)
     y = dot(x, matrix[:half, half:])
     rest = matrix[half:, half:] - dot(matrix[half:, :half], y)
-    between()
-    inner = tail_inverse(rest, 0, half // REG)
+    inner = tail_inverse(rest, 0, half // REG, between)
     t = dot(y, inner)
     top = jnp.concatenate([x + dot(t, y, ((1,), (1,))), -t], axis=1)
     return jnp.concatenate([top, jnp.concatenate([-t.T, inner], axis=1)], axis=0)
@@ -423,13 +438,13 @@
 
 
 def front_kernel(
-    plan, b_hbm, h_ref, v_ref, label_ref, bump_ref, pad_class_ref, edge_table, pad_table,
-    b1_out, b2_out, planes_out, cx_ref, wide_ref,
-    braw, bt, u0, u1, b1, b2, planes, ea, eb, ec, ga, gb, gc, brow, bcol, ccol, cpack, cpack1, beyond,
+    plan, b_hbm, h_hbm, v_hbm, label_hbm, bump_hbm, pad_class_hbm, edge_hbm, pad_hbm,
+    b1_out, b2_out, planes_out, cx_out,
+    h_ref, v_ref, label_ref, bump_ref, pad_class_ref, edge_table, pad_table, braw, bt, u0, u1, b1, b2, planes, ea, eb, ec, ga, gb, gc, brow, bcol, ccol, cpack, cpack1, beyond,
     s0, s1, s2, s3, s4, pa, pb, pc, tacc,
     set0, set1, set2, side0, side1, side2, gset0, gset1, gset2, gside0, gside1, gside2,
-    note, gat, q0, q1, q2, cpad, diag, knat,
-    in_sem, out_sem, send_sem, recv_sem, note_send, note_recv,
+    note, gat, q0, q1, q2, cpad, cpad1, diag, knat, cx_ref,
+    in_sem, small_sem, out_sem, send_sem, recv_sem, note_send, note_recv,
 ):
     rows, cols, n, hn = plan.rows, plan.cols, plan.loads, plan.half
     r, c = lax.axis_index("row"), lax.axis_index("col")
@@ -442,16 +457,22 @@
         return (other // plan.nc, lax.rem(other, plan.nc))
 
     def fetch(k):
-        return pltpu.make_async_copy(b_hbm.at[k], braw.at[pl.ds(pl.multiple_of(k * plan.pitch, 8), rows)], in_sem.at[k])
+        here, there = pl.ds(pl.multiple_of(k * rows, 8), rows), pl.ds(pl.multiple_of(k * plan.pitch, 8), rows)
+        return pltpu.make_async_copy(b_hbm.at[here], braw.at[there], in_sem)
 
     def fetch_start(k, carry):
         fetch(k).start()
         return carry
 
-    def fetch_wait(k, carry):
-        fetch(k).wait()
-        return carry
-
+    small = [
+        pltpu.make_async_copy(src, dst, small_sem.at[k])
+        for k, (src, dst) in enumerate((
+            (h_hbm, h_ref), (edge_hbm, edge_table), (v_hbm, v_ref), (label_hbm, label_ref),
+            (bump_hbm, bump_ref), (pad_class_hbm, pad_class_ref), (pad_hbm, pad_table),
+        ))
+    ]
+    for copy in small:
+        copy.start()
     lax.fori_loop(0, n, fetch_start, 0)
     for ref in (ga, gb, gc, brow, bcol, ccol, gset0, gset1, gset2, gside0, gside1, gside2):
         ref[...] = jnp.zeros_like(ref)
@@ -464,6 +485,8 @@
 
     lax.fori_loop(1, count, greet, 0)
 
+    for copy in small:
+        copy.wait()
     i, j = iota((rows, cols), 0), iota((rows, cols), 1)
     row_end = jnp.where(r == plan.nr - 1, rows - 1, rows)
     col_end = jnp.where(c == plan.nc - 1, cols - 1, cols)
@@ -476,7 +499,7 @@
     put_edges(ea, 2, planes[CO + 1])
     put_edges(ea, 3, planes[CO + 3])
     legs = Legs(plan, send_sem, recv_sem)
-    first_edges = legs.make(beside(ea, ga))
+    first_edges = legs.make(beside(ea, ga), 0)
     base_row, base_col = windows(plan)
     bump = bump_ref[...]
     for k, hit in enumerate(hits_of(label_ref[...].astype(F32), base_row, base_col)):
@@ -486,7 +509,7 @@
 
     for ref in (s0, s1, s2, s3, s4, pa, pb, pc):
         ref[...] = jnp.zeros_like(ref)
-    lax.fori_loop(0, n, fetch_wait, 0)
+    pltpu.make_async_copy(b_hbm, braw.at[pl.ds(0, n * rows)], in_sem).wait()
 
     lane = iota((hn, cols), 1)
     even = lane % 2 == 0
@@ -534,7 +557,7 @@
         (-1, 0, bt.at[pl.ds(0, n)], brow.at[1]),
         (0, 1, cpack.at[0], bcol.at[0]),
         (0, -1, cpack.at[1], bcol.at[1]),
-    ])
+    ], 4)
     legs.start(load_edges)
 
     legs.wait(first_edges)
@@ -567,7 +590,7 @@
         value = total[k] * minv
         planes[V0 + k] = value
         put_edges(eb, 1 + k, value)
-    image_edges = legs.make(beside(eb, gb))
+    image_edges = legs.make(beside(eb, gb), 8)
     legs.start(image_edges)
 
     pair_sums(plan, planes, Z, W0, pa, 0)
@@ -593,8 +616,8 @@
         return pltpu.make_async_remote_copy(
             src_ref=note.at[m],
             dst_ref=gat.at[m, me],
-            send_sem=note_send.at[m, d],
-            recv_sem=note_recv.at[m, d],
+            send_sem=note_send.at[m],
+            recv_sem=note_recv.at[m],
             device_id=device(d),
             device_id_type=pl.DeviceIdType.MESH,
         )
@@ -610,11 +633,17 @@
         lax.fori_loop(1, count, go, 0)
 
     def hear(m):
-        def go(d, carry):
-            note_copy(m, d).wait()
-            return carry
-
-        lax.fori_loop(1, count, go, 0)
+        others = gat.at[m, pl.ds(0, count - 1)]
+        every = pltpu.make_async_remote_copy(
+            src_ref=others,
+            dst_ref=others,
+            send_sem=note_send.at[m],
+            recv_sem=note_recv.at[m],
+            device_id=device(1),
+            device_id_type=pl.DeviceIdType.MESH,
+        )
+        every.wait_recv()
+        every.wait_send()
 
     legs.wait(load_edges)
     legs.wait(image_edges)
@@ -628,7 +657,9 @@
         value = value * planes[MINV]
         planes[V1 + k] = value
         put_edges(ec, k, value)
-    next_edges = legs.make(beside(ec, gc))
+    for gone in (first_edges, load_edges, image_edges):
+        legs.sent(gone)
+    next_edges = legs.make(beside(ec, gc), 0)
     legs.start(next_edges)
 
     def stencil(field, h, k):
@@ -672,7 +703,7 @@
             (-1, 0, u1.at[pl.ds(n + h * hn, hn)], u1.at[pl.ds((rows + 1) * n + h * hn, hn)]),
             (0, 1, cpack1.at[0, mine], ccol.at[0, mine]),
             (0, -1, cpack1.at[1, mine], ccol.at[1, mine]),
-        ]))
+        ], 4 + 4 * h))
         legs.start(field_edges[h])
         if h == 0:
             load_sums, energy = spread0.merged()
@@ -714,11 +745,12 @@
     out2 = pltpu.make_async_copy(b2, b2_out, out_sem.at[2])
     out2.start()
     pair_sums(plan, planes, W2, V1, pc, 0)
+    legs.sent(spread1.mine)
     spread2 = Spread(plan, legs, set2, side2, gset2, gside2)
     spread2.send([packed(plan, pc), packed(plan, s4)])
     dots = jnp.sum(tacc[...].T, axis=0, keepdims=True)
 
-    first_sums, second_sums, third_sums, pairs = spread1.merged()
+    first_sums, second_sums, third_sums, pairs = spread1.merged(True)
     tell(1, message(plan, [(0, first_sums), (1, second_sums), (2, third_sums), (3, pairs)]))
 
     def settle(m, ref):
@@ -740,40 +772,40 @@
     inverse = whole_inverse(coarse_matrix(q0[...], BLOCK), last_message)
     c0 = same(dot(inverse, q0[...]), 0)
     settle(1, q1)
-    settle(2, q2)
+
+    def over(value):
+        return jnp.sum(value, axis=0, keepdims=True)
 
     regions = c0.shape[0]
     block = iota((regions, LANES), 1) // BLOCK
-    pair_values = jnp.where(block == 3, q1[...], q2[...])
-    sums = jnp.where(block == 3, q2[...], q1[...])
-    start = jnp.where(block == 3, 0, 3 * BLOCK + 9 * block)
+    start = 3 * BLOCK + jnp.where(block == 3, 0, 9 * block)
     for k in range(9):
-        diag[k] = taken(pair_values, start + k)
+        diag[k] = taken(q1[...], start + k)
+    for ref in (cpad, cpad1):
+        ref[...] = jnp.zeros_like(ref)
+    cpad[8 : 8 + regions, :] = c0
+    reduced = q1[...] - banded(diag, cpad)
+    solved = dot(inverse, reduced)
+    c1, e2 = same(solved, 0), same(solved, 1)
+    cpad1[8 : 8 + regions, :] = c1
+    image = banded(diag, cpad1)
+    in_c1 = over(c1 * reduced)
+    image_c1 = over(c1 * image)
+    turned = same(dot(inverse, image), 0)
+    settle(2, q2)
+    for k in range(9):
+        diag[k] = jnp.broadcast_to(q2[:, k : k + 1], (regions, LANES))
+    mixed = jnp.where(block == 3, 2.0 * q2[...] - banded(diag, cpad), q1[...] + reduced)
     all_dots = jnp.sum(gat[2], axis=0)
     row_block = iota((1, LANES), 1) // BLOCK
-    dots = jnp.zeros((1, LANES), F32)
+    dots = -over(c0 * mixed)
     for k in range(4):
-        dots = jnp.where(row_block == k, rolled(all_dots[k : k + 1], BLOCK * (k - 1), 1), dots)
-
-    def over(value):
-        return jnp.sum(value, axis=0, keepdims=True)
-
-    cpad[...] = jnp.zeros_like(cpad)
-    cpad[8 : 8 + regions, :] = c0
-    reduced = sums - banded(diag, cpad)
-    dots = dots - over(c0 * (sums + reduced))
+        dots = dots + jnp.where(row_block == k, rolled(all_dots[k : k + 1], BLOCK * (k - 1), 1), 0.0)
     rho, m1, m2, m3 = [same(dots, k) for k in range(4)]
-    solved = dot(inverse, reduced)
-    c1, e2 = same(solved, 0), same(solved, 1)
-    cpad[8 : 8 + regions, :] = c1
-    image = banded(diag, cpad)
-    in_c1 = over(c1 * reduced)
-    image_c1 = over(c1 * image)
     with_s1, with_s2, with_s3 = [same(in_c1, k) for k in range(3)]
     curve = m1 - with_s1
     alpha = rho / curve
     square = m2 - 2.0 * with_s2 + same(image_c1, 0)
-    turned = same(dot(inverse, image), 0)
     c2 = c1 - alpha * (e2 - turned)
     now = reduced - alpha * (pltpu.roll(reduced, 3 * BLOCK, 1) - image)
     in_c2 = same(over(c2 * now), 0)
@@ -785,8 +817,9 @@
     mix = alpha + alpha1 * beta
     kappa, lam = mix + alpha1, alpha * alpha1
     coefs = jnp.where(block == 0, c0 - mix * c1 - alpha1 * c2, jnp.where(block == 1, lam * c1 - kappa * c0, lam * c0))
-    wide_ref[0] = wide(kappa)
-    wide_ref[1] = wide(lam)
+    scales = 6 * plan.levels * n
+    cx_ref[scales : scales + n, :] = wide(kappa)
+    cx_ref[scales + n : scales + 2 * n, :] = wide(lam)
 
     knat[...] = jnp.zeros_like(knat)
     for q in range(REG):
@@ -799,24 +832,33 @@
         for l in range(plan.levels):
             value = taken(near[: 3 * BLOCK], column + l * REG)
             for f in range(3):
-                cx_ref[f, b, l * n : (l + 1) * n, :] = value[f * BLOCK : f * BLOCK + n]
-
+                at = ((2 * f + b) * plan.levels + l) * n
+                cx_ref[at : at + n, :] = value[f * BLOCK : f * BLOCK + n]
+
+    out3 = pltpu.make_async_copy(cx_ref, cx_out, out_sem.at[3])
+    out3.start()
     out0.wait()
     out1.wait()
     out2.wait()
-    legs.finish()
+    out3.wait()
+    legs.sent(next_edges)
+    for gone in field_edges:
+        legs.sent(gone)
 
 
 def last_kernel(
-    plan, b_hbm, b1_hbm, b2_hbm, planes_hbm, cx_ref, wide_ref, x_hbm, r_hbm,
-    braw, b1, b2, planes, xs, rs, in_sem, out_sem,
+    plan, b_hbm, b1_hbm, b2_hbm, planes_hbm, cx_hbm, x_hbm, r_hbm,
+    braw, b1, b2, planes, xs, rs, cx_ref, in_sem, out_sem, cx_sem,
 ):
     n, hn = plan.loads, plan.half
     flat_b = braw.reshape(n * plan.pitch, plan.cols)
     flat_x = xs.reshape(n * plan.pitch, plan.cols)
     flat_r = rs.reshape(n * plan.pitch, plan.cols)
     arrivals, departures = [], []
-    for part, first, last in plan.chunks():
+    spread_copy = pltpu.make_async_copy(cx_hbm, cx_ref, cx_sem)
+    spread_copy.start()
+    pieces = list(plan.pieces())
+    for part, (owner, first, last) in enumerate(pieces):
         here, flat = pl.ds(first, last - first), pl.ds(first * n, (last - first) * n)
         arrivals.append([
             pltpu.make_async_copy(src, dst, in_sem.at[part, k])
@@ -831,20 +873,25 @@
             pltpu.make_async_copy(xs.at[:, here], x_hbm.at[:, here], out_sem.at[part, 0]),
             pltpu.make_async_copy(rs.at[:, here], r_hbm.at[:, here], out_sem.at[part, 1]),
         ])
-    for copies in arrivals:
+    for copies in arrivals[:2]:
         for copy in copies:
             copy.start()
-    for part, first, last in plan.chunks():
+    spread_copy.wait()
+    scales = 6 * plan.levels * n
+    for part, (owner, first, last) in enumerate(pieces):
         for copy in arrivals[part]:
             copy.wait()
+        for copies in arrivals[2:] if part == 0 else ():
+            for copy in copies:
+                copy.start()
         for h in (0, 1):
-            kappa, lam = [wide_ref[k, h * hn : (h + 1) * hn, :] for k in (0, 1)]
+            kappa, lam = [cx_ref[scales + k * n + h * hn : scales + k * n + (h + 1) * hn, :] for k in (0, 1)]
             cx = []
             for f in range(3):
                 for a in (0, 1):
                     for b in (0, 1):
-                        at = (part + a) * n + h * hn
-                        cx.append(cx_ref[f, b, at : at + hn, :])
+                        at = ((2 * f + b) * plan.levels + owner + a) * n + h * hn
+                        cx.append(cx_ref[at : at + hn, :])
 
             def step(k, u, carry):
                 at = pl.ds(pl.multiple_of(k * n + h * hn, 8), hn)
@@ -883,20 +930,28 @@
     tall = ((rows + 2) * n, cols)
     edge = (4, 8, cols)
     sums = (2, LANES, cols)
+    spread = (6 * plan.levels * n + 2 * n, cols)
 
     def vm(*dims):
         return pltpu.VMEM(dims, F32)
 
+    def whole(*dims):
+        return pltpu.VMEM(dims, jnp.int32)
+
+    def sm(dims):
+        return pltpu.SMEM(dims, F32)
+
     def dma(*dims):
         return pltpu.SemaphoreType.DMA(dims)
 
     legs = 4 * 6 + 3 * 8
-    b1, b2, planes, cx, scales = pl.pallas_call(
+    b1, b2, planes, cx = pl.pallas_call(
         functools.partial(front_kernel, plan),
-        out_shape=(shape(*field), shape(*field), shape(KEPT, rows, cols), shape(3, 2, plan.levels * n, cols), shape(2, n, cols)),
-        in_specs=[ANY] + [VM] * 5 + [SM] * 2,
-        out_specs=(ANY, ANY, ANY, VM, VM),
+        out_shape=(shape(*field), shape(*field), shape(KEPT, rows, cols), shape(*spread)),
+        in_specs=[HBM] * 8,
+        out_specs=(HBM,) * 4,
         scratch_shapes=[
+            whole(rows, cols), whole(rows, cols), whole(rows, cols), vm(rows, cols), whole(rows, cols), sm(edge_table.shape), sm(pad_table.shape),
             vm(n * plan.pitch, cols), vm(*field), vm(*tall), vm(*tall), vm(*field), vm(*field), vm(PLANES, rows, cols),
             vm(*edge), vm(*edge), vm(*edge), vm(*edge), vm(*edge), vm(*edge),
             vm(2, n, cols), vm(2, n, cols), vm(2, n, cols), vm(2, n, cols), vm(2, n, cols), vm(*field),
@@ -905,23 +960,23 @@
             vm(2, 8, LANES), vm(4, 8, LANES), vm(2, 8, LANES), vm(2, 8, LANES), vm(2, 8, LANES), vm(2, 8, LANES),
             vm(2, 2, 8, LANES), vm(2, 4, 8, LANES), vm(2, 2, 8, LANES), vm(6, 8, LANES), vm(6, 8, LANES), vm(6, 8, LANES),
             vm(3, 8, LANES), vm(3, count, 8, LANES), vm(regions, LANES), vm(regions, LANES), vm(regions, LANES),
-            vm(regions + 16, LANES), vm(9, regions, LANES), vm(regions + LANES + 2 * REG, LANES),
-            dma(n), dma(3), dma(legs), dma(legs), dma(3, count), dma(3, count),
+            vm(regions + 16, LANES), vm(regions + 16, LANES), vm(9, regions, LANES), vm(regions + LANES + 2 * REG, LANES), vm(*spread),
+            pltpu.SemaphoreType.DMA, dma(7), dma(4), dma(20), dma(legs), dma(3), dma(3),
         ],
         compiler_params=pltpu.CompilerParams(collective_id=0, has_side_effects=True, vmem_limit_bytes=56 * 1024 * 1024),
-    )(load_currents, horizontal_class, vertical_class, labels, bump_height, pad_class, edge_table, pad_table)
+    )(load_currents.reshape(n * rows, cols), horizontal_class, vertical_class, labels, bump_height, pad_class, edge_table, pad_table)
     staged = (n, plan.pitch, cols)
     return pl.pallas_call(
         functools.partial(last_kernel, plan),
         out_shape=(shape(n, rows, cols),) * 2,
-        in_specs=[ANY] * 4 + [VM] * 2,
-        out_specs=(ANY, ANY),
+        in_specs=[HBM] * 5,
+        out_specs=(HBM, HBM),
         scratch_shapes=[
-            vm(*staged), vm(*field), vm(*field), vm(KEPT, rows, cols), vm(*staged), vm(*staged),
-            dma(plan.parts, 4), dma(plan.parts, 2),
+            vm(*staged), vm(*field), vm(*field), vm(KEPT, rows, cols), vm(*staged), vm(*staged), vm(*spread),
+            dma(plan.parts + 2, 4), dma(plan.parts + 2, 2), pltpu.SemaphoreType.DMA,
         ],
         compiler_params=pltpu.CompilerParams(vmem_limit_bytes=56 * 1024 * 1024),
-    )(load_currents, b1, b2, planes, cx, scales)
+    )(load_currents, b1, b2, planes, cx)
 
 
 def solution(mesh):

time: 49.5 us -> 43.9 us (0.89)
  Pallas kernels: 48.5 us -> 42.9 us
    pallas_call x1, Pallas kernels: 39.7 us -> 34 us  [body(): pl.pallas_call(functools.partial(front_kernel, plan), out_shape=(shape(*f...]
where the time goes in v3:
time: 43.9 us; the launch traced here: 43.7 us
  Pallas kernels  42.9 us (98%)
  between operations  0.8 us (2%)
    pallas_call x1, Pallas kernels, body(): pl.pallas_call(functools.partial(front_kernel, plan), out_shape=(shape(*f...  34 us
    pallas_call x1, Pallas kernels, body(): pl.pallas_call(functools.partial(last_kernel, plan), out_shape=(shape(n,...  8.93 us

profile of v3, /device:TPU:0, one launch (start us, length us, event | category | flops | bytes accessed | tf_op | source)
XLA Modules:
  0.0 43.7 jit_solution(15727643903545979454)
XLA Ops:
  0.6 34.0 %shard_map.95 = (f32[4096,128]{1,0:T(8,128)}, f32[4096,128]{1,0:T(8,128)}, f32[17,128,128]{2,1,0:T(8,128)}, f32[832,128]{1,0:T(8,128)}) custom-call(f32[4096,128]{1,0:T(8,128)} %bitcast.1, s32[128,128]{1,0:T(8,128)} %h_hbm.1, s32[128,128]{1,0:T(8,128)} %v_hbm.1, s32[128,128]{1,0:T(8,128)} %label_hbm.1, f32[128,128]{1,0:T(8,128)} %bump_hbm.1, ...), custom_call_target="tpu_custom_call" | custom-call | tf_op jit(solution)/shard_map/pallas_call | solution.py:948
  34.6 8.9 %shard_map.96 = (f32[32,128,128]{2,1,0:T(8,128)}, f32[32,128,128]{2,1,0:T(8,128)}) custom-call(f32[32,128,128]{2,1,0:T(8,128)} %b_hbm.1, f32[4096,128]{1,0:T(8,128)} %get-tuple-element.6.b1_hbm, f32[4096,128]{1,0:T(8,128)} %get-tuple-element.7.b2_hbm, f32[17,128,128]{2,1,0:T(8,128)} %get-tuple-element.8.planes_hbm, f32[832,128]{1,0:T(8,128)} %get-tuple-element.9.cx_hbm), custom_call_target="tpu_custom_call" | custom-call | tf_op jit(solution)/shard_map/pallas_call | solution.py:969

commit v4 on v3

--- a/solution.py
+++ b/solution.py
@@ -15,8 +15,8 @@
 PITCH = 8
 GROUP = 32
 MINV, Z, W0, W1, W2, V0, V1, CO = 0, 1, 5, 9, 13, 17, 21, 25
-KEPT, PLANES = 17, 32
-RIGHT_IN, LEFT_IN = 30, 31
+KEPT, PLANES = 17, 33
+RIGHT_IN, LEFT_IN, OUTER = 30, 31, 32
 ORDER = (0, 2, 4, 6, 8, 10, 12, 14, 1, 5, 9, 13, 3, 11, 7, 15)
 
 
@@ -49,6 +49,12 @@
         half = self.height // 2
         for part in range(self.parts):
             yield part, max(0, part * self.height - half), min(self.rows, part * self.height + half)
+
+    def reached(self, part, first, last):
+        reach, middle = self.height // 4 + 3, part * self.height
+        low, high = (middle - reach) // 4 * 4, -(-(middle + reach) // 4) * 4
+        spans = ((first, min(last, low), (0, 1)), (max(first, low), min(last, high), (0, 1, 2, 3)), (max(first, high), last, (2, 3)))
+        return [span for span in spans if span[1] > span[0]]
 
     def pieces(self):
         for part, first, last in self.chunks():
@@ -439,7 +445,7 @@
 
 def front_kernel(
     plan, b_hbm, h_hbm, v_hbm, label_hbm, bump_hbm, pad_class_hbm, edge_hbm, pad_hbm,
-    b1_out, b2_out, planes_out, cx_out,
+    bt_out, b1_out, b2_out, planes_out, cx_out,
     h_ref, v_ref, label_ref, bump_ref, pad_class_ref, edge_table, pad_table, braw, bt, u0, u1, b1, b2, planes, ea, eb, ec, ga, gb, gc, brow, bcol, ccol, cpack, cpack1, beyond,
     s0, s1, s2, s3, s4, pa, pb, pc, tacc,
     set0, set1, set2, side0, side1, side2, gset0, gset1, gset2, gside0, gside1, gside2,
@@ -559,6 +565,8 @@
         (0, -1, cpack.at[1], bcol.at[1]),
     ], 4)
     legs.start(load_edges)
+    out4 = pltpu.make_async_copy(bt, bt_out, out_sem.at[4])
+    out4.start()
 
     legs.wait(first_edges)
     around = Around(ga, rows, cols)
@@ -646,12 +654,13 @@
         every.wait_send()
 
     legs.wait(load_edges)
+    for h in (0, 1):
+        halo_rows(h, pltpu.roll(bcol[0, own(h), :], 1, 1), bcol[1, own(h), :])
     legs.wait(image_edges)
     u0[0:n, :] = brow[0] * gb[0, 0:1, :]
     u0[(rows + 1) * n :, :] = brow[1] * gb[1, 0:1, :]
-    for h in (0, 1):
-        halo_rows(h, pltpu.roll(bcol[0, own(h), :], 1, 1) * gb[2, 0:1, :], bcol[1, own(h), :] * gb[3, 0:1, :])
     around = Around(gb, rows, cols)
+    planes[OUTER] = jnp.where(j == 0, around.column(2, 0), around.column(3, 0))
     for k, value in enumerate(around.images(plan, planes, V0, 1)):
         planes[W1 + k] = value
         value = value * planes[MINV]
@@ -671,7 +680,7 @@
             - row_of(planes, CO + 3, k) * field[spot(h, k + 2), :]
             - row_of(planes, CO + 4, k) * field[spot(h, k), :]
         )
-        return z, f + beyond[spot(h, k), :]
+        return z, f
 
     field_edges = []
     for h in (0, 1):
@@ -683,6 +692,7 @@
                 for u in range(GROUP):
                     k = base + u
                     z, f = stencil(u0, h, k)
+                    f = f + row_of(planes, OUTER, k) * beyond[spot(h, k), :]
                     w = row_of(planes, MINV, k) * f
                     b1[spot(h, k), :] = f
                     u1[spot(h, k + 1), :] = w
@@ -734,6 +744,7 @@
                 for u in range(GROUP):
                     k = base + u
                     z, f = stencil(u1, h, k)
+                    f = f + beyond[spot(h, k), :]
                     b2[spot(h, k), :] = f
                     dots = dots + z * f
                     acc = tuple(x + row_of(planes, V1 + m, k) * f for m, x in enumerate(acc))
@@ -841,17 +852,17 @@
     out1.wait()
     out2.wait()
     out3.wait()
+    out4.wait()
     legs.sent(next_edges)
     for gone in field_edges:
         legs.sent(gone)
 
 
 def last_kernel(
-    plan, b_hbm, b1_hbm, b2_hbm, planes_hbm, cx_hbm, x_hbm, r_hbm,
-    braw, b1, b2, planes, xs, rs, cx_ref, in_sem, out_sem, cx_sem,
+    plan, bt_hbm, b1_hbm, b2_hbm, planes_hbm, cx_hbm, x_hbm, r_hbm,
+    bt, b1, b2, planes, xs, rs, cx_ref, in_sem, out_sem, cx_sem,
 ):
     n, hn = plan.loads, plan.half
-    flat_b = braw.reshape(n * plan.pitch, plan.cols)
     flat_x = xs.reshape(n * plan.pitch, plan.cols)
     flat_r = rs.reshape(n * plan.pitch, plan.cols)
     arrivals, departures = [], []
@@ -864,7 +875,7 @@
             pltpu.make_async_copy(src, dst, in_sem.at[part, k])
             for k, (src, dst) in enumerate((
                 (planes_hbm.at[:, here], planes.at[:, here]),
-                (b_hbm.at[:, here], braw.at[:, here]),
+                (bt_hbm.at[flat], bt.at[flat]),
                 (b1_hbm.at[flat], b1.at[flat]),
                 (b2_hbm.at[flat], b2.at[flat]),
             ))
@@ -893,14 +904,14 @@
                         at = ((2 * f + b) * plan.levels + owner + a) * n + h * hn
                         cx.append(cx_ref[at : at + hn, :])
 
-            def step(k, u, carry):
+            def step(k, u, carry, seen=()):
                 at = pl.ds(pl.multiple_of(k * n + h * hn, 8), hn)
                 to = pl.ds(k + h * hn * plan.pitch, hn, stride=plan.pitch)
-                v0, v1, v2 = flat_b[to, :], b1[at, :], b2[at, :]
+                v0, v1, v2 = bt[at, :], b1[at, :], b2[at, :]
                 x = kappa * v0 - lam * v1
                 r = v0 - kappa * v1 + lam * v2
                 plain = None
-                for m in range(4):
+                for m in seen:
                     w0 = row_of(planes, W0 + m, k)
                     w1 = row_of(planes, W1 + m, k)
                     x = x + w0 * cx[4 + m] + w1 * cx[8 + m]
@@ -911,7 +922,8 @@
                 flat_r[to, :] = r
                 return carry
 
-            over_rows(first, last, step, 0, 4)
+            for start, stop, seen in plan.reached(owner, first, last):
+                over_rows(start, stop, functools.partial(step, seen=seen), 0, 4)
         for copy in departures[part]:
             copy.start()
     for copies in departures:
@@ -945,11 +957,11 @@
         return pltpu.SemaphoreType.DMA(dims)
 
     legs = 4 * 6 + 3 * 8
-    b1, b2, planes, cx = pl.pallas_call(
+    bt, b1, b2, planes, cx = pl.pallas_call(
         functools.partial(front_kernel, plan),
-        out_shape=(shape(*field), shape(*field), shape(KEPT, rows, cols), shape(*spread)),
+        out_shape=(shape(*field), shape(*field), shape(*field), shape(KEPT, rows, cols), shape(*spread)),
         in_specs=[HBM] * 8,
-        out_specs=(HBM,) * 4,
+        out_specs=(HBM,) * 5,
         scratch_shapes=[
             whole(rows, cols), whole(rows, cols), whole(rows, cols), vm(rows, cols), whole(rows, cols), sm(edge_table.shape), sm(pad_table.shape),
             vm(n * plan.pitch, cols), vm(*field), vm(*tall), vm(*tall), vm(*field), vm(*field), vm(PLANES, rows, cols),
@@ -961,7 +973,7 @@
             vm(2, 2, 8, LANES), vm(2, 4, 8, LANES), vm(2, 2, 8, LANES), vm(6, 8, LANES), vm(6, 8, LANES), vm(6, 8, LANES),
             vm(3, 8, LANES), vm(3, count, 8, LANES), vm(regions, LANES), vm(regions, LANES), vm(regions, LANES),
             vm(regions + 16, LANES), vm(regions + 16, LANES), vm(9, regions, LANES), vm(regions + LANES + 2 * REG, LANES), vm(*spread),
-            pltpu.SemaphoreType.DMA, dma(7), dma(4), dma(20), dma(legs), dma(3), dma(3),
+            pltpu.SemaphoreType.DMA, dma(7), dma(5), dma(20), dma(legs), dma(3), dma(3),
         ],
         compiler_params=pltpu.CompilerParams(collective_id=0, has_side_effects=True, vmem_limit_bytes=56 * 1024 * 1024),
     )(load_currents.reshape(n * rows, cols), horizontal_class, vertical_class, labels, bump_height, pad_class, edge_table, pad_table)
@@ -972,11 +984,11 @@
         in_specs=[HBM] * 5,
         out_specs=(HBM, HBM),
         scratch_shapes=[
-            vm(*staged), vm(*field), vm(*field), vm(KEPT, rows, cols), vm(*staged), vm(*staged), vm(*spread),
+            vm(*field), vm(*field), vm(*field), vm(KEPT, rows, cols), vm(*staged), vm(*staged), vm(*spread),
             dma(plan.parts + 2, 4), dma(plan.parts + 2, 2), pltpu.SemaphoreType.DMA,
         ],
         compiler_params=pltpu.CompilerParams(vmem_limit_bytes=56 * 1024 * 1024),
-    )(load_currents, b1, b2, planes, cx)
+    )(bt, b1, b2, planes, cx)
 
 
 def solution(mesh):

time: 43.9 us -> 42.6 us (0.970)
  Pallas kernels: 42.9 us -> 41.6 us
    pallas_call x1, Pallas kernels: 8.93 us -> 8.19 us  [body(): pl.pallas_call(functools.partial(last_kernel, plan), out_shape=(shape(n,...]
    pallas_call x1, Pallas kernels: 34 us -> 33.4 us  [body(): pl.pallas_call(functools.partial(front_kernel, plan), out_shape=(shape(*f...]
where the time goes in v4:
time: 42.6 us; the launch traced here: 42.4 us
  Pallas kernels  41.6 us (98%)
  between operations  0.8 us (2%)
    pallas_call x1, Pallas kernels, body(): pl.pallas_call(functools.partial(front_kernel, plan), out_shape=(shape(*f...  33.4 us
    pallas_call x1, Pallas kernels, body(): pl.pallas_call(functools.partial(last_kernel, plan), out_shape=(shape(n,...  8.19 us

profile of v4, /device:TPU:0, one launch (start us, length us, event | category | flops | bytes accessed | tf_op | source)
XLA Modules:
  0.0 42.4 jit_solution(9087324053823233589)
XLA Ops:
  0.6 33.4 %shard_map.95 = (f32[4096,128]{1,0:T(8,128)}, f32[4096,128]{1,0:T(8,128)}, f32[4096,128]{1,0:T(8,128)}, f32[17,128,128]{2,1,0:T(8,128)}, f32[832,128]{1,0:T(8,128)}) custom-call(f32[4096,128]{1,0:T(8,128)} %bitcast.1, s32[128,128]{1,0:T(8,128)} %h_hbm.1, s32[128,128]{1,0:T(8,128)} %v_hbm.1, s32[128,128]{1,0:T(8,128)} %label_hbm.1, f32[128,128]{1,0:T(8,128)} %bump_hbm.1, ...), custom_call_target="tpu_custom_call" | custom-call | tf_op jit(solution)/shard_map/pallas_call | solution.py:960
  34.1 8.2 %shard_map.96 = (f32[32,128,128]{2,1,0:T(8,128)}, f32[32,128,128]{2,1,0:T(8,128)}) custom-call(f32[4096,128]{1,0:T(8,128)} %get-tuple-element.7.bt_hbm, f32[4096,128]{1,0:T(8,128)} %get-tuple-element.8.b1_hbm, f32[4096,128]{1,0:T(8,128)} %get-tuple-element.9.b2_hbm, f32[17,128,128]{2,1,0:T(8,128)} %get-tuple-element.10.planes_hbm, ...), custom_call_target="tpu_custom_call" | custom-call | tf_op jit(solution)/shard_map/pallas_call | solution.py:981
